TPU v7x, 32 devices: a whole 2x2x4 slice. The times are simulated.
32 devices in a mesh: member: 2 (over y), slab: 4 (over z), chan: 2 (over x), mode: 2 (over core).
Axes of the slice: x: 2, y: 2, z: 4, core: 2. Of those that a mesh axis runs over, the one named last changes fastest.
Arguments:
- source_field: float32 [128, 1024, 1024], P(('member', 'chan'), 'slab', 'mode'), parts along dimension 0, may hold values from -6 to 6
- cotangent: float32 [128, 1024, 1024], P(('member', 'chan'), 'slab', 'mode'), parts along dimension 0, may hold values from -6 to 6
- spectral_weight: float32 [128, 64, 32, 2, 64], P(('member', 'chan'), None, 'mode', None, 'slab'), parts along dimension 0, may hold values from -12 to 12
- skip_gain: float32 [128], P(('member', 'chan')), parts along dimension 0, may hold values from 0.5 to 2
- channel_bias: float32 [128], P(('member', 'chan')), parts along dimension 0, may hold values from -0.5 to 0.5
- mode_limit: int32 [128, 2], P('member'), parts along dimension 0, may hold values from 16 to 32
- width_limit: int32 [128], P('member'), parts along dimension 0, may hold values from 32 to 64
Outputs:
- output: float32 [128, 1024, 1024], P(('member', 'chan'), 'slab', 'mode'), parts along dimension 0
- field_grad: float32 [128, 1024, 1024], P(('member', 'chan'), 'slab', 'mode'), parts along dimension 0
- spectral_grad: float32 [128, 64, 32, 2, 64], P(('member', 'chan'), None, 'mode', None, 'slab'), parts along dimension 0
- gate_grad: float32 [128], P(('member', 'chan')), parts along dimension 0
- bias_grad: float32 [128], P(('member', 'chan')), parts along dimension 0
There are 2 independent parts, one for each index of `member`. A program takes and returns all parts, laid end to end along the dimension named above; each array names one. Nothing has to cross between parts.
Inputs may be any that keep to these rules, and one draw needn't show every extreme that they name: `mode_limit`: never more than 32. `width_limit`: never more than 64.
All inputs are finite; a program needn't handle non-finite values.
Results may differ from a plain program's by a relative error of at most 0.00018.
Values sent between devices are 32-bit elements; how exact they have to be, the bound alone decides.
A program may use at most 192 MiB of HBM per device.

v0:
```python
import functools
import math

import jax
import jax.numpy as jnp
from jax import lax
from jax.experimental import pallas as pl
from jax.experimental.pallas import tpu as pltpu
from jax.sharding import PartitionSpec as P

LANES = 128
BIG = 60 * 1024 * 1024


def split_table(table):
    high = lax.reduce_precision(table, 8, 7)
    return high.astype(jnp.bfloat16), (table - high).astype(jnp.bfloat16)


def split_block(values):
    high = values.astype(jnp.bfloat16)
    return high, (values - high.astype(jnp.float32)).astype(jnp.bfloat16)


def dot_pair(left, right):
    left_high, left_low = left
    right_high, right_low = right
    mul = functools.partial(jnp.dot, preferred_element_type=jnp.float32)
    return mul(left_high, right_high) + mul(left_low, right_high) + mul(left_high, right_low)


def tables(extent, waves, first_cell, cell_count):
    cell_index = first_cell + jnp.arange(cell_count, dtype=jnp.int32)
    products = (cell_index[:, None] * waves[None, :] % extent).astype(jnp.float32)
    angles = products * (2.0 * math.pi / extent)
    return jnp.cos(angles), jnp.sin(angles)


def store_spectrum(values, col_pair, row_pair, out_ref):
    block, rows, cols = values.shape
    lines = dot_pair(split_block(values.reshape(block * rows, cols)), col_pair)
    all_kx = row_pair[0].shape[0] // 2
    kx, lanes = out_ref.shape[2:]
    span = lanes // block
    mode_count = lines.shape[1] // span
    slabs = out_ref.shape[0] // mode_count
    done = []
    for c in range(block):
        mixed = dot_pair(row_pair, split_block(lines[c * rows : (c + 1) * rows]))
        done.append(mixed[:all_kx] - turn(mixed[all_kx:], span))
    for m in range(mode_count):
        packed = jnp.concatenate([one[:, m * span : (m + 1) * span] for one in done], axis=1)
        for s in range(slabs):
            out_ref[m * slabs + s, 0] = packed[s * kx : (s + 1) * kx]


def turn(values, span):
    half = span // 2
    pieces = []
    for first in range(0, values.shape[1], span):
        pieces.append(-values[:, first + half : first + span])
        pieces.append(values[:, first : first + half])
    return jnp.concatenate(pieces, axis=1)


def all_modes(modes_ref, mode_count, c, block):
    span = modes_ref.shape[3] // block
    slabs = modes_ref.shape[0] // mode_count
    columns = []
    for m in range(mode_count):
        stack = [modes_ref[m * slabs + s, 0] for s in range(slabs)]
        columns.append(jnp.concatenate(stack, axis=0)[:, c * span : (c + 1) * span])
    return jnp.concatenate(columns, axis=1), span


def synth(modes_and_span, row_pair, col_pair):
    modes, span = modes_and_span
    stacked = jnp.concatenate([modes, turn(modes, span)], axis=0)
    lines = dot_pair(row_pair, split_block(stacked))
    return dot_pair(split_block(lines), col_pair)


def spectrum_kernel(x_ref, ch_ref, cl_ref, rh_ref, rl_ref, out_ref):
    store_spectrum(x_ref[...], (ch_ref[...], cl_ref[...]), (rh_ref[...], rl_ref[...]), out_ref)


def middle_kernel(
    mode_count, x_ref, cot_ref, modes_ref, gain_ref, bias_ref, ch_ref, cl_ref, rh_ref, rl_ref,
    cth_ref, ctl_ref, ih_ref, il_ref, out_ref, grad_ref, spec_ref, sums_ref,
):
    block = x_ref.shape[0]
    row_back = (ih_ref[...], il_ref[...])
    col_back = (cth_ref[...], ctl_ref[...])
    scale = math.sqrt(2.0 / math.pi)
    for c in range(block):
        source = x_ref[c]
        gain = gain_ref[c]
        v = synth(all_modes(modes_ref, mode_count, c, block), row_back, col_back) + gain[:, :1] * source + bias_ref[c][:, :1]
        square = v * v
        t = jnp.tanh(scale * v * (1.0 + 0.044715 * square))
        half_up = 0.5 * (1.0 + t)
        out_ref[c] = v * half_up
        slope = half_up + 0.5 * v * (1.0 - t * t) * (scale * (1.0 + 3.0 * 0.044715 * square))
        grad = cot_ref[c] * slope
        grad_ref[c] = grad
        gate = jnp.sum(jnp.sum(grad * source, axis=0, keepdims=True), axis=1, keepdims=True)
        bias = jnp.sum(jnp.sum(grad, axis=0, keepdims=True), axis=1, keepdims=True)
        lane = lax.broadcasted_iota(jnp.int32, (1, LANES), 1)
        sums_ref[c] = jnp.where(lane == 0, gate, bias)
    store_spectrum(
        grad_ref[...], (ch_ref[...], cl_ref[...]), (rh_ref[...], rl_ref[...]), spec_ref
    )


def last_kernel(mode_count, grad_ref, modes_ref, gain_ref, cth_ref, ctl_ref, ih_ref, il_ref, out_ref):
    block = grad_ref.shape[0]
    for c in range(block):
        modes = all_modes(modes_ref, mode_count, c, block)
        branch = synth(modes, (ih_ref[...], il_ref[...]), (cth_ref[...], ctl_ref[...]))
        out_ref[c] = branch + gain_ref[c][:, :1] * grad_ref[c]


def contract_kernel(w_ref, spec_ref, limit_ref, out_ref):
    block, freqs, _, kx, outs = w_ref.shape
    first = lax.axis_index("chan") * (block * pl.num_programs(0)) + pl.program_id(0) * block

    @pl.when(pl.program_id(0) == 0)
    def _():
        out_ref[...] = jnp.zeros_like(out_ref)

    limit = limit_ref[...]
    for y in range(freqs):
        real = out_ref[y, 0]
        imag = out_ref[y, 1]
        for i in range(block):
            keep = first + i < limit
            spec = spec_ref[0]
            at = 2 * freqs * i + y
            s_real = jnp.where(keep, spec[:, at : at + 1], 0.0)
            s_imag = jnp.where(keep, spec[:, freqs + at : freqs + at + 1], 0.0)
            w_real = w_ref[i, y, 0]
            w_imag = w_ref[i, y, 1]
            real = real + (s_real * w_real - s_imag * w_imag)
            imag = imag + (s_real * w_imag + s_imag * w_real)
        out_ref[y, 0] = real
        out_ref[y, 1] = imag


def back_kernel(w_ref, spec_ref, grads_ref, limit_ref, wgrad_ref, out_ref):
    block, freqs, _, kx, outs = w_ref.shape
    first = lax.axis_index("chan") * (block * pl.num_programs(0)) + pl.program_id(0) * block
    limit = limit_ref[...]
    lane = lax.broadcasted_iota(jnp.int32, out_ref.shape[1:], 1)
    spec = spec_ref[0]
    back = jnp.zeros(out_ref.shape[1:], jnp.float32)
    for i in range(block):
        keep = first + i < limit
        for y in range(freqs):
            at = 2 * freqs * i + y
            g_real = jnp.where(keep, grads_ref[y, 0], 0.0)
            g_imag = jnp.where(keep, grads_ref[y, 1], 0.0)
            s_real = spec[:, at : at + 1]
            s_imag = spec[:, freqs + at : freqs + at + 1]
            wgrad_ref[i, y, 0] = s_real * g_real + s_imag * g_imag
            wgrad_ref[i, y, 1] = s_real * g_imag - s_imag * g_real
            w_real = w_ref[i, y, 0]
            w_imag = w_ref[i, y, 1]
            b_real = jnp.sum(g_real * w_real + g_imag * w_imag, axis=1, keepdims=True)
            b_imag = jnp.sum(g_imag * w_real - g_real * w_imag, axis=1, keepdims=True)
            back = jnp.where(lane == at, b_real, back)
            back = jnp.where(lane == freqs + at, b_imag, back)
    out_ref[0] = back


def exchange_kernel(axes, sizes, gather, x_ref, out_ref, send_sem, recv_sem, own_sem):
    total = math.prod(sizes)
    me = lax.axis_index(axes[0])
    for axis, size in zip(axes[1:], sizes[1:]):
        me = me * size + lax.axis_index(axis)

    def place(index):
        coords = {}
        for axis, size in reversed(list(zip(axes, sizes))):
            coords[axis] = lax.rem(index, size)
            index = lax.div(index, size)
        return coords

    barrier = pltpu.get_barrier_semaphore()
    for step in range(1, total):
        pl.semaphore_signal(
            barrier, inc=1, device_id=place(lax.rem(me + step, total)),
            device_id_type=pl.DeviceIdType.MESH,
        )
    pl.semaphore_wait(barrier, total - 1)
    copies = []
    for step in range(1, total):
        peer = lax.rem(me + step, total)
        copy = pltpu.make_async_remote_copy(
            src_ref=x_ref if gather else x_ref.at[peer],
            dst_ref=out_ref.at[me],
            send_sem=send_sem.at[step],
            recv_sem=recv_sem.at[step],
            device_id=place(peer),
            device_id_type=pl.DeviceIdType.MESH,
        )
        copy.start()
        copies.append(copy)
    own = pltpu.make_async_copy(x_ref if gather else x_ref.at[me], out_ref.at[me], own_sem)
    own.start()
    own.wait()
    for copy in copies:
        copy.wait()


def exchange(values, axes, gather, ident):
    sizes = tuple(lax.axis_size(axis) for axis in axes)
    total = math.prod(sizes)
    piece = values.shape if gather else values.shape[1:]
    flat = values.reshape((-1, LANES) if gather else (total, -1, LANES))
    out = pl.pallas_call(
        functools.partial(exchange_kernel, axes, sizes, gather),
        out_shape=jax.ShapeDtypeStruct((total,) + flat.shape[-2:], jnp.float32),
        in_specs=[pl.BlockSpec(memory_space=pltpu.VMEM)],
        out_specs=pl.BlockSpec(memory_space=pltpu.VMEM),
        scratch_shapes=[
            pltpu.SemaphoreType.DMA((total,)),
            pltpu.SemaphoreType.DMA((total,)),
            pltpu.SemaphoreType.DMA,
        ],
        compiler_params=pltpu.CompilerParams(collective_id=ident, has_side_effects=True),
        name="exchange" + str(ident),
    )(flat)
    return out.reshape((total,) + piece)


def mode_weights(limit_rows, col_freq, row_freq, kx_count, cells_total):
    keep_cols = col_freq[None, :] < limit_rows[:, 0:1]
    keep_rows = (row_freq[None, :] < limit_rows[:, 1:2]) | (
        (kx_count - row_freq)[None, :] < limit_rows[:, 1:2]
    )
    scales = jnp.where(col_freq == 0, 1.0, 2.0).astype(jnp.float32) / cells_total
    joined = keep_rows[:, :, None] & keep_cols[:, None, :]
    return (joined.astype(jnp.float32) * scales[None, None, :])[:, :, None, :]


def local(
    source_field, cotangent, spectral_weight, skip_gain, channel_bias, mode_limit, width_limit
):
    channels, row_count, col_count = source_field.shape
    slabs = lax.axis_size("slab")
    modes = lax.axis_size("mode")
    chans = lax.axis_size("chan")
    slab_index = lax.axis_index("slab")
    mode_index = lax.axis_index("mode")
    chan_index = lax.axis_index("chan")
    outs = spectral_weight.shape[1]
    freqs = spectral_weight.shape[2]
    kx = spectral_weight.shape[4]
    all_freqs = freqs * modes
    all_kx = kx * slabs
    all_rows = row_count * slabs
    all_cols = col_count * modes

    col_waves = jnp.arange(all_freqs, dtype=jnp.int32)
    row_waves = jnp.arange(all_kx, dtype=jnp.int32)
    row_waves = row_waves + jnp.where(2 * row_waves >= all_kx, all_rows - all_kx, 0)
    col_cos, col_sin = tables(all_cols, col_waves, mode_index * col_count, col_count)
    row_cos, row_sin = tables(all_rows, row_waves, slab_index * row_count, row_count)
    col_tab = jnp.stack(
        [col_cos.reshape(-1, modes, freqs), -col_sin.reshape(-1, modes, freqs)], axis=2
    ).reshape(col_count, 2 * all_freqs)
    row_tab = jnp.concatenate([row_cos, row_sin], axis=1)
    col_pair = split_table(col_tab)
    col_back = tuple(part.T for part in col_pair)
    row_back = split_table(row_tab)
    row_pair = tuple(part.T for part in row_back)

    block = LANES // (2 * freqs)
    groups = channels // block
    owners = slabs * modes
    cells = pl.BlockSpec((block, row_count, col_count), lambda c: (c, 0, 0))
    freq_cells = pl.BlockSpec((owners, 1, kx, LANES), lambda c: (0, c, 0, 0))
    per_channel = pl.BlockSpec((block, 1, LANES), lambda c: (c, 0, 0))
    field = jax.ShapeDtypeStruct(source_field.shape, jnp.float32)
    freq_field = jax.ShapeDtypeStruct((owners, groups, kx, LANES), jnp.float32)
    params = pltpu.CompilerParams(
        dimension_semantics=("arbitrary",), vmem_limit_bytes=BIG
    )

    def whole(array):
        return pl.BlockSpec(array.shape, lambda c: (0,) * array.ndim)

    grid = (channels // block,)
    wide = lambda values: jnp.broadcast_to(values[:, None, None], (channels, 1, LANES))
    gain = wide(skip_gain)
    forward = col_pair + row_pair
    back = col_back + row_back

    def spread(partial, ident):
        half = exchange(partial.reshape(modes, -1, LANES), ("mode",), False, ident)
        half = jnp.sum(half, axis=0).reshape(slabs, -1, LANES)
        return jnp.sum(exchange(half, ("slab",), False, ident + 1), axis=0).reshape(
            groups, kx, LANES
        )

    def joined(piece, ident):
        half = exchange(piece, ("slab",), True, ident)
        return exchange(half, ("mode",), True, ident + 1).reshape((owners,) + piece.shape)

    spectra = spread(
        pl.pallas_call(
            spectrum_kernel,
            grid=grid,
            in_specs=[cells] + [whole(t) for t in forward],
            out_specs=freq_cells,
            out_shape=freq_field,
            compiler_params=params,
            name="spectrum",
        )(source_field, *forward),
        0,
    )

    weight = spectral_weight.transpose(0, 2, 3, 4, 1)
    limit = width_limit.reshape(1, outs)
    in_block = block
    w_spec = pl.BlockSpec((in_block, freqs, 2, kx, outs), lambda i: (i, 0, 0, 0, 0))
    s_spec = pl.BlockSpec((1, kx, LANES), lambda i: (i, 0, 0))
    mode_spec = pl.BlockSpec((freqs, 2, kx, outs), lambda i: (0, 0, 0, 0))
    limit_spec = pl.BlockSpec((1, outs), lambda i: (0, 0))
    partial_modes = pl.pallas_call(
        contract_kernel,
        grid=(channels // in_block,),
        in_specs=[w_spec, s_spec, limit_spec],
        out_specs=mode_spec,
        out_shape=jax.ShapeDtypeStruct((freqs, 2, kx, outs), jnp.float32),
        compiler_params=params,
        name="contract",
    )(weight, spectra, limit)
    halves = partial_modes.reshape(freqs, 2, kx, chans, groups, block)
    halves = halves.transpose(3, 4, 2, 5, 1, 0).reshape(chans, groups, kx, LANES)
    summed_modes = jnp.sum(exchange(halves, ("chan",), False, 2), axis=0)

    col_freq = mode_index * freqs + jnp.arange(freqs, dtype=jnp.int32)
    row_freq = slab_index * kx + jnp.arange(kx, dtype=jnp.int32)
    limit_rows = lax.dynamic_slice_in_dim(mode_limit, chan_index * channels, channels, 0)
    weights = mode_weights(limit_rows, col_freq, row_freq, all_kx, all_rows * all_cols)
    weights = jnp.broadcast_to(weights, (channels, kx, 2, freqs))
    weights = weights.reshape(groups, block, kx, 2 * freqs).transpose(0, 2, 1, 3)
    weights = weights.reshape(groups, kx, LANES)
    out_modes = joined(summed_modes * weights, 3)

    output, grad_sum, grad_partial, sums = pl.pallas_call(
        functools.partial(middle_kernel, modes),
        grid=grid,
        in_specs=[cells, cells, freq_cells, per_channel, per_channel]
        + [whole(t) for t in forward + back],
        out_specs=[cells, cells, freq_cells, per_channel],
        out_shape=[
            field,
            field,
            freq_field,
            jax.ShapeDtypeStruct((channels, 1, LANES), jnp.float32),
        ],
        compiler_params=params,
        name="middle",
    )(source_field, cotangent, out_modes, gain, wide(channel_bias), *forward, *back)

    grad_modes = spread(grad_partial, 5) * weights
    all_grads = exchange(grad_modes, ("chan",), True, 7)
    all_grads = all_grads.reshape(chans, groups, kx, block, 2, freqs)
    all_grads = all_grads.transpose(5, 4, 2, 0, 1, 3).reshape(freqs, 2, kx, outs)
    weight_grad, back_modes = pl.pallas_call(
        back_kernel,
        grid=(channels // in_block,),
        in_specs=[w_spec, s_spec, mode_spec, limit_spec],
        out_specs=[w_spec, s_spec],
        out_shape=[
            jax.ShapeDtypeStruct(weight.shape, jnp.float32),
            jax.ShapeDtypeStruct(spectra.shape, jnp.float32),
        ],
        compiler_params=params,
        name="back",
    )(weight, spectra, all_grads, limit)
    spectral_grad = weight_grad.transpose(0, 4, 1, 2, 3)

    sent = back_modes.size // LANES
    row_sums = sums[:, 0, :2].T.reshape(-1)
    extra = -(-row_sums.size // (8 * LANES)) * 8
    row_sums = jnp.pad(row_sums, (0, extra * LANES - row_sums.size)).reshape(extra, LANES)
    packed = jnp.concatenate([back_modes.reshape(sent, LANES), row_sums], axis=0)
    parts = joined(packed, 8)
    field_modes = parts[:, :sent].reshape(owners, groups, kx, LANES)
    totals = jnp.sum(parts[:, sent:], axis=0).reshape(-1)
    gate_grad = totals[:channels]
    bias_grad = totals[channels : 2 * channels]
    field_grad = pl.pallas_call(
        functools.partial(last_kernel, modes),
        grid=grid,
        in_specs=[cells, freq_cells, per_channel] + [whole(t) for t in back],
        out_specs=cells,
        out_shape=field,
        compiler_params=params,
        name="last",
    )(grad_sum, field_modes, gain, *back)
    return (output, field_grad, spectral_grad, gate_grad, bias_grad)


def solution(mesh):
    in_specs = (
        P(("member", "chan"), "slab", "mode"),
        P(("member", "chan"), "slab", "mode"),
        P(("member", "chan"), None, "mode", None, "slab"),
        P(("member", "chan")),
        P(("member", "chan")),
        P("member", None),
        P("member"),
    )
    out_specs = (
        P(("member", "chan"), "slab", "mode"),
        P(("member", "chan"), "slab", "mode"),
        P(("member", "chan"), None, "mode", None, "slab"),
        P(("member", "chan")),
        P(("member", "chan")),
    )
    return jax.shard_map(local, mesh=mesh, in_specs=in_specs, out_specs=out_specs, check_vma=False)
```

profile of v0, /device:TPU:0, one launch (start us, length us, event | category | flops | bytes accessed | tf_op | source)
XLA Modules:
  0.0 207.0 jit_solution(7463916735803346383)
XLA Ops:
  0.6 0.0 copy-start
  0.7 0.7 copy-done
  1.3 0.1 constant_dynamic-slice_fusion
  1.5 0.1 compare_or_fusion
  1.6 1.4 broadcast_in_dim.27.gain_ref
  2.9 1.3 broadcast_in_dim.28.bias_ref
  4.3 0.3 fusion.10
  4.6 0.0 copy-start.2
  4.7 0.0 copy-start.3
  4.7 0.8 copy.24.cl_ref
  5.4 0.8 copy.23.ch_ref
  6.2 0.1 and_select_fusion
  6.3 0.6 fusion.9
  6.9 0.1 fusion.1
  7.0 0.0 copy-start.4
  7.0 0.0 copy-start.5
  7.1 0.7 copy.25.rh_ref
  7.8 0.7 copy.26.rl_ref
  8.5 0.3 broadcast_in_dim.26
  8.8 0.3 reshape.298
  9.1 0.1 copy.29
  9.2 0.2 reshape.299
  9.4 15.8 %spectrum.1 = f32[8,8,16,128]{3,2,1,0:T(8,128)} custom-call(f32[32,256,512]{2,1,0:T(8,128)} %x_ref.3, bf16[512,64]{1,0:T(8,128)(2,1)} %copy.23.ch_ref, bf16[512,64]{1,0:T(8,128)(2,1)} %copy.24.cl_ref, bf16[128,256]{1,0:T(8,128)(2,1)} %copy.25.rh_ref, bf16[128,256]{1,0:T(8,128)(2,1)} %copy.26.rl_ref), custom_call_target="tpu_custom_call" | custom-call | tf_op jit(solution)/shard_map/spectrum/pallas_call | solution.py:311
  25.1 3.6 %exchange0.1 = f32[2,512,128]{2,1,0:T(8,128)} custom-call(f32[2,512,128]{2,1,0:T(8,128)} %bitcast.47), custom_call_target="tpu_custom_call" | custom-call | tf_op jit(solution)/shard_map/exchange0/pallas_call | solution.py:220
  28.7 1.8 reduce_sum.54
  30.5 12.1 %exchange1.1 = f32[4,128,128]{2,1,0:T(8,128)} custom-call(f32[4,128,128]{2,1,0:T(8,128)} %bitcast.57), custom_call_target="tpu_custom_call" | custom-call | tf_op jit(solution)/shard_map/exchange1/pallas_call | solution.py:220
  42.6 1.6 reduce_sum.55
  44.2 8.4 %contract.1 = f32[16,2,16,64]{3,2,1,0:T(8,128)} custom-call(f32[32,16,2,16,64]{4,3,2,1,0:T(8,128)} %bitcast.39, f32[8,16,128]{2,1,0:T(8,128)} %bitcast.59, s32[1,64]{1,0:T(1,128)} %bitcast.65), custom_call_target="tpu_custom_call" | custom-call | tf_op jit(solution)/shard_map/contract/pallas_call | solution.py:330
  52.6 1.4 copy.27
  54.0 0.0 copy-done.2
  54.1 0.0 copy-done.3
  54.1 0.8 copy.28
  54.9 0.0 copy-done.4
  54.9 0.0 copy-done.5
  54.9 2.0 reshape_reshape.15.x_ref
  56.8 5.8 %exchange2.1 = f32[2,128,128]{2,1,0:T(8,128)} custom-call(f32[2,128,128]{2,1,0:T(8,128)} %reshape_reshape.15.x_ref), custom_call_target="tpu_custom_call" | custom-call | tf_op jit(solution)/shard_map/exchange2/pallas_call | solution.py:220
  62.7 0.9 reduce_sum.56
  63.6 0.6 mul.133.x_ref
  64.3 9.6 %exchange3.1 = f32[4,128,128]{2,1,0:T(8,128)} custom-call(f32[128,128]{1,0:T(8,128)} %mul.133.x_ref), custom_call_target="tpu_custom_call" | custom-call | tf_op jit(solution)/shard_map/exchange3/pallas_call | solution.py:220
  73.8 3.3 %exchange4.1 = f32[2,512,128]{2,1,0:T(8,128)} custom-call(f32[512,128]{1,0:T(8,128)} %bitcast.55), custom_call_target="tpu_custom_call" | custom-call | tf_op jit(solution)/shard_map/exchange4/pallas_call | solution.py:220
  77.2 41.4 %middle.1 = (f32[32,256,512]{2,1,0:T(8,128)}, f32[32,256,512]{2,1,0:T(8,128)}, f32[8,8,16,128]{3,2,1,0:T(8,128)}, f32[32,1,128]{2,1,0:T(1,128)}) custom-call(f32[32,256,512]{2,1,0:T(8,128)} %x_ref.3, f32[32,256,512]{2,1,0:T(8,128)} %cot_ref.1, f32[8,8,16,128]{3,2,1,0:T(8,128)} %bitcast.45, f32[32,1,128]{2,1,0:T(1,128)} %broadcast_in_dim.27.gain_ref, ...), custom_call_target="tpu_custom_call" | custom-call | tf_op jit(solution)/shard_map/middle/pallas_call | solution.py:352
  118.6 0.8 copy.36
  119.4 0.1 reshape.304
  119.5 3.4 %exchange5.1 = f32[2,512,128]{2,1,0:T(8,128)} custom-call(f32[2,512,128]{2,1,0:T(8,128)} %bitcast.61), custom_call_target="tpu_custom_call" | custom-call | tf_op jit(solution)/shard_map/exchange5/pallas_call | solution.py:220
  122.9 1.8 reduce_sum.57
  124.7 10.5 %exchange6.1 = f32[4,128,128]{2,1,0:T(8,128)} custom-call(f32[4,128,128]{2,1,0:T(8,128)} %bitcast.58), custom_call_target="tpu_custom_call" | custom-call | tf_op jit(solution)/shard_map/exchange6/pallas_call | solution.py:220
  135.3 1.0 reduce_sum.58
  136.3 0.6 mul.134.x_ref
  136.9 5.8 %exchange7.1 = f32[2,128,128]{2,1,0:T(8,128)} custom-call(f32[128,128]{1,0:T(8,128)} %mul.134.x_ref), custom_call_target="tpu_custom_call" | custom-call | tf_op jit(solution)/shard_map/exchange7/pallas_call | solution.py:220
  142.7 2.2 %reshape_reshape.18 = f32[2,8,16,4,2,16]{5,4,3,2,1,0:T(2,128)S(1)} reshape(f32[2,128,128]{2,1,0:T(8,128)} %exchange7.1) | data formatting | bytes 262144 | tf_op jit(solution)/shard_map/reshape;reshape | solution.py:370
  144.9 0.5 copy.34
  145.5 1.2 copy.35.grads_ref
  146.7 24.0 %back.1 = (f32[32,16,2,16,64]{4,3,2,1,0:T(8,128)}, f32[8,16,128]{2,1,0:T(8,128)}) custom-call(f32[32,16,2,16,64]{4,3,2,1,0:T(8,128)} %bitcast.40, f32[8,16,128]{2,1,0:T(8,128)} %bitcast.60, f32[16,2,16,64]{3,2,1,0:T(8,128)} %copy.35.grads_ref, s32[1,64]{1,0:T(1,128)} %bitcast.66), custom_call_target="tpu_custom_call" | custom-call | tf_op jit(solution)/shard_map/back/pallas_call | solution.py:372
  170.7 1.5 pad_maximum_fusion.2.x_ref
  172.2 9.8 %exchange8.1 = f32[4,136,128]{2,1,0:T(8,128)} custom-call(f32[136,128]{1,0:T(8,128)} %pad_maximum_fusion.2.x_ref), custom_call_target="tpu_custom_call" | custom-call | tf_op jit(solution)/shard_map/exchange8/pallas_call | solution.py:220
  181.9 3.4 %exchange9.1 = f32[2,544,128]{2,1,0:T(8,128)} custom-call(f32[544,128]{1,0:T(8,128)} %bitcast.48), custom_call_target="tpu_custom_call" | custom-call | tf_op jit(solution)/shard_map/exchange9/pallas_call | solution.py:220
  185.3 0.8 slice_reduce_fusion
  186.1 1.9 slice.32
  187.9 0.0 copy-start.1
  187.9 18.4 %last.1 = f32[32,256,512]{2,1,0:T(8,128)} custom-call(f32[32,256,512]{2,1,0:T(8,128)} %get-tuple-element.12.grad_ref, f32[8,8,16,128]{3,2,1,0:T(8,128)} %bitcast.46, f32[32,1,128]{2,1,0:T(1,128)} %broadcast_in_dim.27.gain_ref, bf16[64,512]{1,0:T(8,128)(2,1)} %bitcast.52, bf16[64,512]{1,0:T(8,128)(2,1)} %bitcast.50, bf16[256,128]{1,0:T(8,128)(2,1)} %copy-done.5, ...), custom_call_target="tpu_custom_call" | custom-call | tf_op jit(solution)/shard_map/last/pallas_call | solution.py:396
  206.4 0.6 fusion.12
  207.0 0.0 copy-done.1
  (12 shorter events, 0.1 us)
Async XLA Ops:
  0.6 0.7 copy-start
  4.6 49.4 %copy-start.2 = (bf16[512,64]{0,1:T(8,128)(2,1)}, bf16[512,64]{0,1:T(8,128)(2,1)S(1)}, u32[]{:S(2)}) copy-start(bf16[512,64]{0,1:T(8,128)(2,1)S(1)} %get-tuple-element.19) | copy-start | bytes 196612
  4.7 49.4 %copy-start.3 = (bf16[512,64]{0,1:T(8,128)(2,1)}, bf16[512,64]{0,1:T(8,128)(2,1)S(1)}, u32[]{:S(2)}) copy-start(bf16[512,64]{0,1:T(8,128)(2,1)S(1)} %get-tuple-element.20) | copy-start | bytes 196612
  7.0 47.8 %copy-start.4 = (bf16[256,128]{1,0:T(8,128)(2,1)}, bf16[256,128]{1,0:T(8,128)(2,1)S(1)}, u32[]{:S(2)}) copy-start(bf16[256,128]{1,0:T(8,128)(2,1)S(1)} %get-tuple-element.17.il_ref) | copy-start | bytes 196612
  7.0 47.8 %copy-start.5 = (bf16[256,128]{1,0:T(8,128)(2,1)}, bf16[256,128]{1,0:T(8,128)(2,1)S(1)}, u32[]{:S(2)}) copy-start(bf16[256,128]{1,0:T(8,128)(2,1)S(1)} %get-tuple-element.18.ih_ref) | copy-start | bytes 196612
  187.9 19.0 %copy-start.1 = (s32[64,2]{0,1:T(2,128)S(1)}, s32[64,2]{0,1:T(2,128)}, u32[]{:S(2)}) copy-start(s32[64,2]{0,1:T(2,128)} %param.12) | copy-start | bytes 1540
where the time goes:
time: 208 us; the launch traced here: 207 us
  Pallas kernels  175 us (84%)
  local copies, waits for them, and re-layouts  18.8 us (9%)
  other arithmetic  11.9 us (6%)
    pallas_call x10, Pallas kernels, exchange(): pl.pallas_call(functools.partial(exchange_kernel, axes, sizes, gather), o...  67.3 us
    pallas_call x1, Pallas kernels, local(): pl.pallas_call(functools.partial(middle_kernel, modes), grid=grid, in_spe...  41.4 us
    pallas_call x1, Pallas kernels, local(): pl.pallas_call(back_kernel, grid=(channels // in_block,), in_specs=[w_spe...  24 us
    pallas_call x1, Pallas kernels, local(): pl.pallas_call(functools.partial(last_kernel, modes), grid=grid, in_specs...  18.4 us
    pallas_call x1, Pallas kernels, local(): pl.pallas_call(spectrum_kernel, grid=grid, in_specs=[cells] + [whole(t) f...  15.8 us
    pallas_call x1, Pallas kernels, local(): pl.pallas_call(contract_kernel, grid=(channels // in_block,), in_specs=[w...  8.39 us

commit v1 on v0

--- a/solution.py
+++ b/solution.py
@@ -3,6 +3,8 @@
 
 import jax
 import jax.numpy as jnp
+import ml_dtypes
+import numpy as np
 from jax import lax
 from jax.experimental import pallas as pl
 from jax.experimental.pallas import tpu as pltpu
@@ -243,7 +245,7 @@
     return (joined.astype(jnp.float32) * scales[None, None, :])[:, :, None, :]
 
 
-def local(
+def local_plain(
     source_field, cotangent, spectral_weight, skip_gain, channel_bias, mode_limit, width_limit
 ):
     channels, row_count, col_count = source_field.shape
@@ -405,6 +407,568 @@
     return (output, field_grad, spectral_grad, gate_grad, bias_grad)
 
 
+def halves_of(table):
+    table = table.astype(np.float32)
+    high = table.astype(ml_dtypes.bfloat16)
+    low = (table - high.astype(np.float32)).astype(ml_dtypes.bfloat16)
+    return high, low
+
+
+def packed_tables(all_rows, all_cols, slabs, modes, freqs, kx_all):
+    cell = np.arange(all_cols)[:, None]
+    angle = (cell * np.arange(modes * freqs)[None, :] % all_cols) * (2.0 * np.pi / all_cols)
+    parts = np.stack([np.cos(angle), -np.sin(angle)], axis=1).reshape(modes, -1, 2, modes, freqs)
+    parts = parts.transpose(0, 1, 3, 2, 4)
+    cols = parts.shape[1]
+    high, low = halves_of(parts)
+    ahead = np.stack([high, low], axis=3).reshape(modes, cols, -1)
+    ahead = np.concatenate([ahead, ahead], axis=1)
+    flat_high = high.reshape(modes, cols, -1).transpose(0, 2, 1)
+    flat_low = low.reshape(modes, cols, -1).transpose(0, 2, 1)
+    behind = np.concatenate([flat_high, flat_low, flat_high, flat_low], axis=1)
+    wave = np.arange(kx_all)
+    wave = wave + np.where(2 * wave >= kx_all, all_rows - kx_all, 0)
+    angle = (np.arange(all_rows)[:, None] * wave[None, :] % all_rows) * (2.0 * np.pi / all_rows)
+    table = np.concatenate([np.cos(angle), np.sin(angle)], axis=1).reshape(slabs, -1, 2 * kx_all)
+    high, low = halves_of(table)
+    row_behind = np.concatenate([high, high, low], axis=2)
+    high, low = high.transpose(0, 2, 1), low.transpose(0, 2, 1)
+    row_ahead = np.concatenate([high, low, high], axis=2)
+    return ahead, row_ahead, row_behind, behind
+
+
+def lane_roll(values, shift):
+    shift = shift % values.shape[-1]
+    return values if shift == 0 else pltpu.roll(values, shift, values.ndim - 1)
+
+
+def lanes_of(shape):
+    return lax.broadcasted_iota(jnp.int32, shape, len(shape) - 1)
+
+
+def high_low(values):
+    high = values.astype(jnp.bfloat16)
+    return high, (values - high.astype(jnp.float32)).astype(jnp.bfloat16)
+
+
+def quarter_turn(values, span, sign):
+    half = span // 2
+    first = lanes_of(values.shape) % span < half
+    back, ahead = lane_roll(values, -half), lane_roll(values, half)
+    return jnp.where(first, -back, ahead) if sign > 0 else jnp.where(first, back, -ahead)
+
+
+def mix_rows(lines, row_table, rows, span, out_ref, kx):
+    block = LANES // span
+    mixed = []
+    for c in range(0, block, 2):
+        pair = jnp.concatenate([lines[c * rows : (c + 1) * rows], lines[(c + 1) * rows : (c + 2) * rows]], axis=1)
+        high, low = high_low(pair)
+        both = jnp.dot(row_table, jnp.concatenate([high, high, low], axis=0), preferred_element_type=jnp.float32)
+        mixed += [both[:, :LANES], both[:, LANES:]]
+    lane = lanes_of(mixed[0].shape)
+    pairs = []
+    for c in range(0, block, 2):
+        left = mixed[c] + lane_roll(mixed[c], -span)
+        right = mixed[c + 1] + lane_roll(mixed[c + 1], span)
+        pairs.append(jnp.where(lane % (2 * span) < span, left, right))
+    low_half = lane < LANES // 2
+    owners = [
+        jnp.where(low_half, pairs[0], lane_roll(pairs[1], LANES // 2)),
+        jnp.where(low_half, lane_roll(pairs[0], LANES // 2), pairs[1]),
+    ]
+    all_kx = owners[0].shape[0] // 2
+    slabs = all_kx // kx
+    for m, values in enumerate(owners):
+        done = values[:all_kx] + quarter_turn(values[all_kx:], span, -1)
+        for s in range(slabs):
+            out_ref[m * slabs + s, 0] = done[s * kx : (s + 1) * kx]
+
+
+def spectrum_packed(span, x_ref, ahead_ref, row_ref, out_ref):
+    block, rows, cols = x_ref.shape
+    high, low = high_low(x_ref[...].reshape(block * rows, cols))
+    lines = jnp.dot(jnp.concatenate([high, low], axis=1), ahead_ref[0], preferred_element_type=jnp.float32)
+    mix_rows(lines, row_ref[0], rows, span, out_ref, out_ref.shape[2])
+
+
+def group_lines(modes_ref, row_table, span):
+    block = LANES // span
+    owners = modes_ref.shape[0]
+    half = owners // 2
+    stack = []
+    for m in range(2):
+        stack.append(jnp.concatenate([modes_ref[m * half + s, 0] for s in range(half)], axis=0))
+    full = [jnp.concatenate([one, quarter_turn(one, span, 1)], axis=0) for one in stack]
+    rolled = [[lane_roll(one, k * span) for k in range(block)] for one in full]
+    lane = lanes_of(full[0].shape)
+    even = lane % (2 * span) < span
+    low_half = lane < LANES // 2
+    sides = []
+    for c in range(block):
+        first = jnp.where(low_half, rolled[0][(0 - c) % block], rolled[0][(2 - c) % block])
+        second = jnp.where(low_half, rolled[1][(1 - c) % block], rolled[1][(3 - c) % block])
+        sides.append(jnp.where(even, first, second))
+    lines = []
+    for c in range(0, block, 2):
+        high, low = high_low(jnp.concatenate([sides[c], sides[c + 1]], axis=1))
+        both = jnp.dot(row_table, jnp.concatenate([high, low, high], axis=0), preferred_element_type=jnp.float32)
+        lines += [both[:, :LANES], both[:, LANES:]]
+    return lines
+
+
+def branch_of(lines, behind):
+    high, low = high_low(lines)
+    return jnp.dot(jnp.concatenate([high, low], axis=1), behind, preferred_element_type=jnp.float32)
+
+
+def middle_packed(
+    span, x_ref, cot_ref, modes_ref, gain_ref, bias_ref, ahead_ref, row_ref, row_back_ref, behind_ref,
+    out_ref, grad_ref, spec_ref, sums_ref, split_ref,
+):
+    block, rows, cols = x_ref.shape
+    step = pl.program_id(0)
+    scale = math.sqrt(2.0 / math.pi)
+
+    @pl.when(step == 0)
+    def _():
+        sums_ref[...] = jnp.zeros_like(sums_ref)
+
+    lines = group_lines(modes_ref, row_back_ref[0], span)
+    lane = lanes_of(sums_ref.shape)
+    line = lax.broadcasted_iota(jnp.int32, sums_ref.shape, 0)
+    for c in range(block):
+        source = x_ref[c]
+        v = branch_of(lines[c], behind_ref[0]) + (gain_ref[step * block + c] * source + bias_ref[step * block + c])
+        square = v * v
+        inner = v * (scale + (scale * 0.044715) * square)
+        up = 0.5 + 0.5 * jnp.tanh(inner)
+        out_ref[c] = v * up
+        bend = v * (2.0 * scale + (6.0 * scale * 0.044715) * square)
+        grad = cot_ref[c] * (up + (up * (1.0 - up)) * bend)
+        grad_ref[c] = grad
+        high, low = high_low(grad)
+        split_ref[c * rows : (c + 1) * rows, :cols] = high
+        split_ref[c * rows : (c + 1) * rows, cols:] = low
+        gate = jnp.sum(jnp.sum(grad * source, axis=0, keepdims=True), axis=1, keepdims=True)
+        bias = jnp.sum(jnp.sum(grad, axis=0, keepdims=True), axis=1, keepdims=True)
+        here = (lane == step * block + c) & (line < 2)
+        sums_ref[...] = jnp.where(here, jnp.where(line == 0, gate, bias), sums_ref[...])
+    made = jnp.dot(split_ref[...], ahead_ref[0], preferred_element_type=jnp.float32)
+    mix_rows(made, row_ref[0], rows, span, spec_ref, spec_ref.shape[2])
+
+
+def last_packed(span, grad_ref, modes_ref, gain_ref, row_back_ref, behind_ref, out_ref):
+    block = grad_ref.shape[0]
+    step = pl.program_id(0)
+    lines = group_lines(modes_ref, row_back_ref[0], span)
+    for c in range(block):
+        out_ref[c] = branch_of(lines[c], behind_ref[0]) + gain_ref[step * block + c] * grad_ref[c]
+
+
+def swap_groups(values, kx):
+    lane = lanes_of(values.shape) // kx
+    line = lax.broadcasted_iota(jnp.int32, values.shape, 1)
+    count = values.shape[1]
+    hop = 1
+    while hop < count:
+        up = lane_roll(pltpu.roll(values, count - hop, 1), hop * kx)
+        down = lane_roll(pltpu.roll(values, hop, 1), -hop * kx)
+        lane_bit, line_bit = lane // hop % 2, line // hop % 2
+        values = jnp.where(lane_bit == line_bit, values, jnp.where(lane_bit == 1, up, down))
+        hop *= 2
+    return values
+
+
+def to_lanes(packed, out_ref, kx):
+    lines = swap_groups(packed.T.reshape(-1, 8, LANES), kx)
+    wide = out_ref.shape[0]
+    block = lines.shape[0] // wide
+    for c in range(block):
+        for j in range(wide):
+            out_ref[j, pl.ds(c, 8, stride=block)] = lines[c * wide + j]
+
+
+def to_rows(wide_ref, block, kx):
+    wide = wide_ref.shape[0]
+    pieces = []
+    for c in range(block):
+        for j in range(wide):
+            pieces.append(wide_ref[j, pl.ds(c, 8, stride=block)][None])
+    return swap_groups(jnp.concatenate(pieces, axis=0), kx).reshape(-1, LANES).T
+
+
+def both_parts(ref, rows):
+    half = ref.shape[0] // 2
+    parts = [jnp.concatenate([ref[p * half + j, rows] for j in range(half)], axis=1) for p in range(2)]
+    return parts[0], parts[1]
+
+
+def put_part(ref, rows, part, values):
+    half = ref.shape[0] // 2
+    for j in range(half):
+        ref[part * half + j, rows] = values[:, j * LANES : (j + 1) * LANES]
+
+
+def other(axis, step, size):
+    return lax.rem(lax.axis_index(axis) + step, size)
+
+
+def send(source, target, sends, recvs, axis, peer):
+    copy = pltpu.make_async_remote_copy(
+        src_ref=source, dst_ref=target, send_sem=sends, recv_sem=recvs,
+        device_id={axis: peer}, device_id_type=pl.DeviceIdType.MESH,
+    )
+    copy.start()
+    return copy
+
+
+def greet(slabs):
+    barrier = pltpu.get_barrier_semaphore()
+    targets = [("mode", 1, 2), ("chan", 1, 2)] + [("slab", step, slabs) for step in range(1, slabs)]
+    for axis, step, size in targets:
+        pl.semaphore_signal(
+            barrier, inc=1, device_id={axis: other(axis, step, size)}, device_id_type=pl.DeviceIdType.MESH
+        )
+    pl.semaphore_wait(barrier, len(targets))
+
+
+def scatter_sum(part_ref, half_ref, give_ref, take_ref, mode_sems, slab_sems, slabs, between):
+    me_mode, me_slab = lax.axis_index("mode"), lax.axis_index("slab")
+    peer = other("mode", 1, 2)
+    order = [slabs // 2] + [step for step in range(1, slabs) if step != slabs // 2] + [0]
+    copies = []
+    for step in order:
+        slab = other("slab", step, slabs)
+        copies.append(send(
+            part_ref.at[peer * slabs + slab], half_ref.at[step], mode_sems.at[0, step], mode_sems.at[1, step], "mode", peer
+        ))
+    waits = list(copies)
+    out = []
+    for step, copy in zip(order, copies):
+        copy.wait_recv()
+        slab = other("slab", step, slabs)
+        total = part_ref[me_mode * slabs + slab] + half_ref[step]
+        if step == 0:
+            mine = total
+        else:
+            give_ref[step] = total
+            out.append(send(
+                give_ref.at[step], take_ref.at[step], slab_sems.at[0, step], slab_sems.at[1, step], "slab", slab
+            ))
+    between()
+    for copy in out:
+        copy.wait_recv()
+    for step in range(1, slabs):
+        mine = mine + take_ref[step]
+    return mine, [copy.wait_send for copy in copies + out]
+
+
+def gather_start(own_ref, out_ref, mode_sems, slab_sems, slabs):
+    me = lax.axis_index("mode") * slabs + lax.axis_index("slab")
+    copies = []
+    for step in [slabs // 2] + [step for step in range(1, slabs) if step != slabs // 2]:
+        copies.append(send(
+            own_ref, out_ref.at[me], slab_sems.at[0, step], slab_sems.at[1, step], "slab", other("slab", step, slabs)
+        ))
+    near = send(own_ref, out_ref.at[me], mode_sems.at[0, 0], mode_sems.at[1, 0], "mode", other("mode", 1, 2))
+    out_ref[me] = own_ref[...]
+    return copies, near
+
+
+def gather_finish(state, out_ref, mode_sems, slabs, between):
+    copies, near = state
+    relays = []
+    order = [slabs // 2] + [step for step in range(1, slabs) if step != slabs // 2]
+    for k in list(range(1, slabs - 1)) + [0]:
+        between(k)
+        copies[k].wait_recv()
+        step = order[k]
+        source = lax.axis_index("mode") * slabs + other("slab", slabs - step, slabs)
+        relays.append(send(
+            out_ref.at[source], out_ref.at[source], mode_sems.at[0, step], mode_sems.at[1, step], "mode", other("mode", 1, 2)
+        ))
+    near.wait()
+    for copy in relays:
+        copy.wait()
+    for copy in copies:
+        copy.wait_send()
+
+
+def forward_kernel(
+    slabs, kx, part_ref, w_ref, limit_ref, weight_ref, out_ref, turned_ref, spec_ref,
+    half_ref, give_ref, take_ref, w_buf, t_buf, sum_ref, peer_ref, own_ref,
+    mode_a, slab_a, mode_b, slab_b, chan_sems, w_sems, t_sems,
+):
+    ins, freqs = w_ref.shape[0], w_ref.shape[1]
+    outs = w_ref.shape[4]
+    mine_outs = outs // 2
+    wide = freqs * kx
+    for i in range(ins):
+        pltpu.make_async_copy(w_ref.at[i], w_buf.at[i], w_sems.at[i]).start()
+    greet(slabs)
+    first = lax.axis_index("chan") * ins
+
+    def flip():
+        def body(i, carry):
+            pltpu.make_async_copy(w_ref.at[i], w_buf.at[i], w_sems.at[i]).wait()
+            keep = jnp.broadcast_to(limit_ref[:, :1], (outs, wide)) > first + i
+            for p in range(2):
+                turned = w_buf[i, :, p].reshape(wide, outs).T
+                t_buf[i, :, p * wide : (p + 1) * wide] = jnp.where(keep, turned, 0.0)
+            pltpu.make_async_copy(t_buf.at[i], turned_ref.at[i], t_sems.at[i]).start()
+            return carry
+        lax.fori_loop(0, ins, body, 0)
+
+    mine, sent = scatter_sum(part_ref, half_ref, give_ref, take_ref, mode_a, slab_a, slabs, flip)
+    to_lanes(mine, spec_ref, kx)
+
+    def contract(i, carry):
+        real, imag = carry
+        w_real, w_imag = t_buf[i, :, :wide], t_buf[i, :, wide:]
+        s_real, s_imag = both_parts(spec_ref, pl.ds(i, 1))
+        return real + (s_real * w_real - s_imag * w_imag), imag + (s_real * w_imag + s_imag * w_real)
+
+    zero = jnp.zeros((outs, wide), jnp.float32)
+    real, imag = lax.fori_loop(0, ins, contract, (zero, zero))
+    put_part(sum_ref, slice(None), 0, real)
+    put_part(sum_ref, slice(None), 1, imag)
+    theirs = other("chan", 1, 2) * mine_outs
+    swap = send(
+        sum_ref.at[:, pl.ds(theirs, mine_outs)], peer_ref, chan_sems.at[0], chan_sems.at[1], "chan", other("chan", 1, 2)
+    )
+    swap.wait_recv()
+    for j in range(peer_ref.shape[0]):
+        peer_ref[j] = (sum_ref[j, pl.ds(first, mine_outs)] + peer_ref[j]) * weight_ref[j % weight_ref.shape[0]]
+    own_ref[...] = to_rows(peer_ref, mine_outs // 8, kx)
+    state = gather_start(own_ref, out_ref, mode_b, slab_b, slabs)
+    gather_finish(state, out_ref, mode_b, slabs, lambda k: None)
+    swap.wait_send()
+    for wait in sent:
+        wait()
+
+    def settle(i, carry):
+        pltpu.make_async_copy(t_buf.at[i], turned_ref.at[i], t_sems.at[i]).wait()
+        return carry
+    lax.fori_loop(0, ins, settle, 0)
+
+
+def backward_kernel(
+    slabs, kx, part_ref, sums_ref, turned_ref, spec_ref, limit_ref, weight_ref,
+    out_ref, wgrad_ref, total_ref,
+    half_ref, give_ref, take_ref, g_buf, t_buf, grad_ref, back_ref, own_ref, near_ref, far_ref, pass_ref,
+    mode_a, slab_a, mode_b, slab_b, chan_sems, g_sems, t_sems, sum_mode, sum_slab,
+):
+    ins, freqs = wgrad_ref.shape[0], wgrad_ref.shape[1]
+    outs = wgrad_ref.shape[4]
+    mine_outs = outs // 2
+    wide = freqs * kx
+    for i in range(ins):
+        pltpu.make_async_copy(turned_ref.at[i], t_buf.at[i], t_sems.at[i]).start()
+    greet(slabs)
+    first = lax.axis_index("chan") * ins
+    near = send(sums_ref, near_ref, sum_mode.at[0], sum_mode.at[1], "mode", other("mode", 1, 2))
+
+    far = []
+    def total_up():
+        near.wait_recv()
+        pass_ref[...] = sums_ref[...] + near_ref[...]
+        for step in range(1, slabs):
+            far.append(send(
+                pass_ref, far_ref.at[step], sum_slab.at[0, step], sum_slab.at[1, step], "slab", other("slab", step, slabs)
+            ))
+
+    mine, sent = scatter_sum(part_ref, half_ref, give_ref, take_ref, mode_a, slab_a, slabs, total_up)
+    to_lanes(mine, back_ref, kx)
+    here = pl.ds(first, mine_outs)
+    for j in range(back_ref.shape[0]):
+        grad_ref[j, here] = back_ref[j] * weight_ref[j % weight_ref.shape[0]]
+    swap = send(
+        grad_ref.at[:, here], grad_ref.at[:, here], chan_sems.at[0], chan_sems.at[1], "chan", other("chan", 1, 2)
+    )
+
+    def arrive(i, carry):
+        pltpu.make_async_copy(turned_ref.at[i], t_buf.at[i], t_sems.at[i]).wait()
+        return carry
+    lax.fori_loop(0, ins, arrive, 0)
+    swap.wait_recv()
+
+    def pull(i, carry):
+        w_real, w_imag = t_buf[i, :, :wide], t_buf[i, :, wide:]
+        g_real, g_imag = both_parts(grad_ref, slice(None))
+        put_part(back_ref, pl.ds(i, 1), 0, jnp.sum(g_real * w_real + g_imag * w_imag, axis=0, keepdims=True))
+        put_part(back_ref, pl.ds(i, 1), 1, jnp.sum(g_imag * w_real - g_real * w_imag, axis=0, keepdims=True))
+        return carry
+    lax.fori_loop(0, ins, pull, 0)
+    own_ref[...] = to_rows(back_ref, ins // 8, kx)
+    state = gather_start(own_ref, out_ref, mode_b, slab_b, slabs)
+    share = ins // (slabs - 1)
+
+    def outer(i, carry):
+        keep = jnp.broadcast_to(limit_ref[:, :1], (outs, wide)) > first + i
+        g_real, g_imag = both_parts(grad_ref, slice(None))
+        s_real, s_imag = both_parts(spec_ref, pl.ds(i, 1))
+        real = jnp.where(keep, s_real * g_real + s_imag * g_imag, 0.0)
+        imag = jnp.where(keep, s_real * g_imag - s_imag * g_real, 0.0)
+        g_buf[i, :, 0] = real.T.reshape(freqs, kx, outs)
+        g_buf[i, :, 1] = imag.T.reshape(freqs, kx, outs)
+        pltpu.make_async_copy(g_buf.at[i], wgrad_ref.at[i], g_sems.at[i]).start()
+        return carry
+
+    done = [0]
+    def between(k):
+        stop = ins if k == 0 else done[0] + share
+        lax.fori_loop(done[0], stop, outer, 0)
+        done[0] = stop
+
+    gather_finish(state, out_ref, mode_b, slabs, between)
+    total = pass_ref[...]
+    for step, copy in zip(range(1, slabs), far):
+        copy.wait()
+        total = total + far_ref[step]
+    total_ref[...] = total
+    near.wait_send()
+    swap.wait_send()
+    for wait in sent:
+        wait()
+
+    def settle(i, carry):
+        pltpu.make_async_copy(g_buf.at[i], wgrad_ref.at[i], g_sems.at[i]).wait()
+        return carry
+    lax.fori_loop(0, ins, settle, 0)
+
+
+def fits(shapes, mesh_sizes):
+    channels, rows, cols = shapes[0]
+    outs, freqs, kx = shapes[2][1], shapes[2][2], shapes[2][4]
+    slabs, modes, chans = mesh_sizes
+    return (
+        modes == 2 and chans == 2 and slabs > 2 and slabs % 2 == 0
+        and 8 * kx == LANES and 8 * freqs == LANES and 2 * freqs * channels == 8 * LANES
+        and outs == chans * channels
+        and rows % LANES == 0 and cols % LANES == 0
+    )
+
+
+def local(source_field, cotangent, spectral_weight, skip_gain, channel_bias, mode_limit, width_limit):
+    slabs, modes, chans = (lax.axis_size(axis) for axis in ("slab", "mode", "chan"))
+    args = (source_field, cotangent, spectral_weight, skip_gain, channel_bias, mode_limit, width_limit)
+    if not fits([one.shape for one in args], (slabs, modes, chans)):
+        return local_plain(*args)
+    channels, rows, cols = source_field.shape
+    outs, freqs, kx = spectral_weight.shape[1], spectral_weight.shape[2], spectral_weight.shape[4]
+    span = 2 * freqs
+    block = LANES // span
+    groups = channels // block
+    owners = slabs * modes
+    all_kx, all_rows, all_cols = kx * slabs, rows * slabs, cols * modes
+    wide = freqs * kx
+    ahead, row_ahead, row_behind, behind = (
+        jnp.asarray(t) for t in packed_tables(all_rows, all_cols, slabs, modes, freqs, all_kx)
+    )
+    slab_index, mode_index, chan_index = (lax.axis_index(axis) for axis in ("slab", "mode", "chan"))
+
+    def pick(table, axis):
+        return pl.BlockSpec((1,) + table.shape[1:], lambda g: (lax.axis_index(axis), 0, 0))
+
+    cells = pl.BlockSpec((block, rows, cols), lambda g: (g, 0, 0))
+    freq_cells = pl.BlockSpec((owners, 1, kx, LANES), lambda g: (0, g, 0, 0))
+    scalars = pl.BlockSpec(memory_space=pltpu.SMEM)
+    small = pl.BlockSpec((8, LANES), lambda g: (0, 0))
+    field = jax.ShapeDtypeStruct(source_field.shape, jnp.float32)
+    freq_field = jax.ShapeDtypeStruct((owners, groups, kx, LANES), jnp.float32)
+    params = pltpu.CompilerParams(dimension_semantics=("arbitrary",), vmem_limit_bytes=BIG)
+    f32 = jnp.float32
+
+    partial = pl.pallas_call(
+        functools.partial(spectrum_packed, span),
+        grid=(groups,),
+        in_specs=[cells, pick(ahead, "mode"), pick(row_ahead, "slab")],
+        out_specs=freq_cells,
+        out_shape=freq_field,
+        compiler_params=params,
+        name="spectrum",
+    )(source_field, ahead, row_ahead)
+
+    weight = spectral_weight.transpose(0, 2, 3, 4, 1)
+    col_freq = mode_index * freqs + jnp.arange(freqs, dtype=jnp.int32)
+    row_freq = slab_index * kx + jnp.arange(kx, dtype=jnp.int32)
+    limit_rows = lax.dynamic_slice_in_dim(mode_limit, chan_index * channels, channels, 0)
+    flat_cols, flat_rows = jnp.repeat(col_freq, kx)[None, :], jnp.tile(row_freq, freqs)[None, :]
+    kept = (flat_cols < limit_rows[:, 0:1]) & (
+        (flat_rows < limit_rows[:, 1:2]) | (all_kx - flat_rows < limit_rows[:, 1:2])
+    )
+    scales = jnp.where(flat_cols == 0, 1.0, 2.0).astype(jnp.float32) / (all_rows * all_cols)
+    weights = jnp.where(kept, scales, 0.0).reshape(channels, -1, LANES).transpose(1, 0, 2)
+    limit = jnp.broadcast_to(width_limit[:, None], (outs, LANES))
+
+    dma, vmem = pltpu.SemaphoreType.DMA, pltpu.VMEM
+    in_vmem, anywhere = pl.BlockSpec(memory_space=pltpu.VMEM), pl.BlockSpec(memory_space=pl.ANY)
+    piece = (groups * kx, LANES)
+    common = [vmem((slabs,) + piece, f32), vmem((slabs,) + piece, f32), vmem((slabs,) + piece, f32)]
+    pair = [dma((2, slabs))] * 4
+    comm = lambda ident: pltpu.CompilerParams(collective_id=ident, has_side_effects=True, vmem_limit_bytes=BIG)
+    gathered = jax.ShapeDtypeStruct((owners,) + piece, f32)
+    flat = lambda lines: (2 * wide // LANES, lines, LANES)
+    turned_shape = jax.ShapeDtypeStruct((channels, outs, 2 * wide), f32)
+
+    out_modes, turned, spec = pl.pallas_call(
+        functools.partial(forward_kernel, slabs, kx),
+        in_specs=[in_vmem, anywhere, in_vmem, in_vmem],
+        out_specs=[in_vmem, anywhere, in_vmem],
+        out_shape=[gathered, turned_shape, jax.ShapeDtypeStruct(flat(channels), f32)],
+        scratch_shapes=common + [
+            vmem(weight.shape, f32), vmem(turned_shape.shape, f32), vmem(flat(outs), f32),
+            vmem(flat(outs // 2), f32), vmem(piece, f32),
+        ] + pair + [dma((2,)), dma((channels,)), dma((channels,))],
+        compiler_params=comm(20),
+        name="forward_modes",
+    )(partial.reshape((owners,) + piece), weight, limit, weights)
+
+    output, grad_sum, grad_partial, sums = pl.pallas_call(
+        functools.partial(middle_packed, span),
+        grid=(groups,),
+        in_specs=[
+            cells, cells, freq_cells, scalars, scalars, pick(ahead, "mode"), pick(row_ahead, "slab"),
+            pick(row_behind, "slab"), pick(behind, "mode"),
+        ],
+        out_specs=[cells, cells, freq_cells, small],
+        out_shape=[field, field, freq_field, jax.ShapeDtypeStruct((8, LANES), f32)],
+        scratch_shapes=[vmem((block * rows, 2 * cols), jnp.bfloat16)],
+        compiler_params=params,
+        name="middle",
+    )(
+        source_field, cotangent, out_modes.reshape(freq_field.shape), skip_gain, channel_bias,
+        ahead, row_ahead, row_behind, behind,
+    )
+
+    back_modes, weight_grad, totals = pl.pallas_call(
+        functools.partial(backward_kernel, slabs, kx),
+        in_specs=[in_vmem, in_vmem, anywhere, in_vmem, in_vmem, in_vmem],
+        out_specs=[in_vmem, anywhere, in_vmem],
+        out_shape=[gathered, jax.ShapeDtypeStruct(weight.shape, f32), jax.ShapeDtypeStruct((8, LANES), f32)],
+        scratch_shapes=common + [
+            vmem(weight.shape, f32), vmem(turned_shape.shape, f32), vmem(flat(outs), f32),
+            vmem(flat(channels), f32), vmem(piece, f32), vmem((8, LANES), f32),
+            vmem((slabs, 8, LANES), f32), vmem((8, LANES), f32),
+        ] + pair + [dma((2,)), dma((channels,)), dma((channels,)), dma((2,)), dma((2, slabs))],
+        compiler_params=comm(21),
+        name="backward_modes",
+    )(grad_partial.reshape((owners,) + piece), sums, turned, spec, limit, weights)
+    spectral_grad = weight_grad.transpose(0, 4, 1, 2, 3)
+
+    field_grad = pl.pallas_call(
+        functools.partial(last_packed, span),
+        grid=(groups,),
+        in_specs=[cells, freq_cells, scalars, pick(row_behind, "slab"), pick(behind, "mode")],
+        out_specs=cells,
+        out_shape=field,
+        compiler_params=params,
+        name="last",
+    )(grad_sum, back_modes.reshape(freq_field.shape), skip_gain, row_behind, behind)
+    return (output, field_grad, spectral_grad, totals[0, :channels], totals[1, :channels])
+
+
 def solution(mesh):
     in_specs = (
         P(("member", "chan"), "slab", "mode"),

time: 208 us -> 133 us (0.64)
  Pallas kernels: 175 us -> 119 us
  other arithmetic: 11.9 us -> 0.71 us
  local copies, waits for them, and re-layouts: 18.8 us -> 12 us
    pallas_call x15 -> x5, Pallas kernels: 175 us -> 119 us  [the longest x1 31.7 us: local(): pl.pallas_call(functools.partial(middle_packed, span), grid=(groups,), in...]
    unnamed x12 -> x5, local copies, waits for them, and re-layouts: 0.69 us -> 9.03 us
    reduce_sum x6 -> x0, other arithmetic: 7.86 us -> none  [the longest x2 3.6 us: spread(): half = jnp.sum(half, axis=0).reshape(slabs, -1, LANES)]
    another operation x3 -> x2, local copies, waits for them, and re-layouts: 4.71 us -> 0.08 us  [local(): jnp.tile(row_freq, freqs)[None, :]]
    slice x4 -> x0, local copies, waits for them, and re-layouts: 3.25 us -> none  [the longest x1 1.87 us: local(): field_modes = parts[:, :sent].reshape(owners, groups, kx, LANES)]
    transpose x4 -> x0, local copies, waits for them, and re-layouts: 2.37 us -> none  [the longest x2 1.46 us: local(): row_pair = tuple((part.T for part in row_back))]
where the time goes in v1:
time: 133 us
  Pallas kernels  119 us (89%)
  local copies, waits for them, and re-layouts  12 us (9%)
    pallas_call x1, Pallas kernels, local(): pl.pallas_call(functools.partial(middle_packed, span), grid=(groups,), in...  31.7 us
    pallas_call x1, Pallas kernels, local(): pl.pallas_call(functools.partial(forward_kernel, slabs, kx), in_specs=[in...  28.9 us
    pallas_call x1, Pallas kernels, local(): pl.pallas_call(functools.partial(backward_kernel, slabs, kx), in_specs=[i...  28.3 us
    pallas_call x1, Pallas kernels, local(): pl.pallas_call(functools.partial(last_packed, span), grid=(groups,), in_s...  16.7 us
    pallas_call x1, Pallas kernels, local(): pl.pallas_call(functools.partial(spectrum_packed, span), grid=(groups,),...  13.7 us
    unnamed x5, local copies, waits for them, and re-layouts  9.03 us

profile of v1, /device:TPU:0, one launch (start us, length us, event | category | flops | bytes accessed | tf_op | source)
XLA Modules:
  0.0 132.7 jit_solution(14383289599825625613)
XLA Ops:
  0.6 0.0 copy-start
  0.7 0.7 copy-done
  1.3 0.1 constant_dynamic-slice_fusion
  1.4 0.1 tile.9
  1.5 0.1 broadcast_in_dim.32
  1.6 0.1 broadcast_in_dim.33
  1.7 0.7 and_select_fusion.weight_ref
  2.3 1.3 %broadcast_in_dim.31.limit_ref = s32[64,128]{1,0:T(8,128)} broadcast(s32[64]{0:T(128)} %param.17), dimensions={0} | broadcast | bytes 33024 | tf_op jit(solution)/shard_map/broadcast_in_dim | solution.py:903
  3.7 13.7 %spectrum.1 = f32[8,8,16,128]{3,2,1,0:T(8,128)} custom-call(f32[32,256,512]{2,1,0:T(8,128)} %x_ref.3, bf16[2,1024,128]{2,1,0:T(8,128)(2,1)} %constant.40.clone.ahead_ref, bf16[4,128,768]{2,1,0:T(8,128)(2,1)} %constant.41.clone.row_ref), custom_call_target="tpu_custom_call" | custom-call | tf_op jit(solution)/shard_map/spectrum/pallas_call | solution.py:883
  17.4 28.9 %forward_modes.1 = (f32[8,128,128]{2,1,0:T(8,128)}, f32[32,64,512]{2,1,0:T(8,128)}, f32[4,32,128]{2,1,0:T(8,128)}) custom-call(f32[8,128,128]{2,1,0:T(8,128)} %bitcast.16, f32[32,16,2,16,64]{4,3,2,1,0:T(8,128)} %bitcast.14, s32[64,128]{1,0:T(8,128)} %broadcast_in_dim.31.limit_ref, f32[2,32,128]{2,1,0:T(8,128)} %and_select_fusion.weight_ref), custom_call_target="tpu_custom_call" | custom-call | tf_op jit(solution)/shard_map/forward_modes/pallas_call | solution.py:915
  46.3 31.7 %middle.1 = (f32[32,256,512]{2,1,0:T(8,128)}, f32[32,256,512]{2,1,0:T(8,128)}, f32[8,8,16,128]{3,2,1,0:T(8,128)}, f32[8,128]{1,0:T(8,128)}) custom-call(f32[32,256,512]{2,1,0:T(8,128)} %x_ref.3, f32[32,256,512]{2,1,0:T(8,128)} %cot_ref.1, f32[8,8,16,128]{3,2,1,0:T(8,128)} %bitcast.18, f32[32]{0:T(128)} %gain_ref.3, f32[32]{0:T(128)} %bias_ref.1, ...), custom_call_target="tpu_custom_call" | custom-call | tf_op jit(solution)/shard_map/middle/pallas_call | solution.py:928
  78.0 28.3 %backward_modes.1 = (f32[8,128,128]{2,1,0:T(8,128)}, f32[32,16,2,16,64]{4,3,2,1,0:T(8,128)}, f32[8,128]{1,0:T(8,128)}) custom-call(f32[8,128,128]{2,1,0:T(8,128)} %bitcast.19, f32[8,128]{1,0:T(8,128)} %get-tuple-element.19.sums_ref, f32[32,64,512]{2,1,0:T(8,128)} %get-tuple-element.20.turned_ref, f32[4,32,128]{2,1,0:T(8,128)} %get-tuple-element.21.spec_ref, ...), custom_call_target="tpu_custom_call" | custom-call | tf_op jit(solution)/shard_map/backward_modes/pallas_call | solution.py:945
  106.3 0.0 copy-start.1
  106.3 16.7 %last.1 = f32[32,256,512]{2,1,0:T(8,128)} custom-call(f32[32,256,512]{2,1,0:T(8,128)} %get-tuple-element.17.grad_ref, f32[8,8,16,128]{3,2,1,0:T(8,128)} %bitcast.17, f32[32]{0:T(128)} %gain_ref.3, bf16[4,256,384]{2,1,0:T(8,128)(2,1)} %constant.42.clone.row_back_ref, bf16[2,256,512]{2,1,0:T(8,128)(2,1)} %constant.43.clone.behind_ref), custom_call_target="tpu_custom_call" | custom-call | tf_op jit(solution)/shard_map/last/pallas_call | solution.py:960
  123.0 1.3 slice_bitcast_fusion
  124.3 8.4 %copy.17 = f32[32,64,16,2,16]{1,4,3,2,0:T(8,128)} copy(f32[32,64,16,2,16]{1,4,3,2,0:T(8,128)} %bitcast.15) | data formatting | bytes 8388608
  132.7 0.0 copy-done.1
  (6 shorter events, 0.0 us)
Async XLA Ops:
  0.6 0.7 copy-start
  106.3 26.4 %copy-start.1 = (s32[64,2]{0,1:T(2,128)S(1)}, s32[64,2]{0,1:T(2,128)}, u32[]{:S(2)}) copy-start(s32[64,2]{0,1:T(2,128)} %param.16) | copy-start | bytes 1540

commit v2 on v1

--- a/solution.py
+++ b/solution.py
@@ -12,6 +12,7 @@
 
 LANES = 128
 BIG = 60 * 1024 * 1024
+MIB = 1024 * 1024
 
 
 def split_table(table):
@@ -546,7 +547,7 @@
         out_ref[c] = v * up
         bend = v * (2.0 * scale + (6.0 * scale * 0.044715) * square)
         grad = cot_ref[c] * (up + (up * (1.0 - up)) * bend)
-        grad_ref[c] = grad
+        grad_ref[step * block + c] = grad
         high, low = high_low(grad)
         split_ref[c * rows : (c + 1) * rows, :cols] = high
         split_ref[c * rows : (c + 1) * rows, cols:] = low
@@ -558,12 +559,25 @@
     mix_rows(made, row_ref[0], rows, span, spec_ref, spec_ref.shape[2])
 
 
-def last_packed(span, grad_ref, modes_ref, gain_ref, row_back_ref, behind_ref, out_ref):
-    block = grad_ref.shape[0]
+def last_packed(
+    span, kx, grad_ref, modes_ref, gain_ref, row_back_ref, behind_ref, grads_ref, spec_ref, limit_ref, out_ref, wgrad_ref
+):
+    block = out_ref.shape[0]
     step = pl.program_id(0)
     lines = group_lines(modes_ref, row_back_ref[0], span)
+    count, freqs, outs = wgrad_ref.shape[0], wgrad_ref.shape[1], wgrad_ref.shape[4]
+    wide = freqs * kx
+    first = lax.axis_index("chan") * (count * pl.num_programs(0)) + step * count
+    g_real, g_imag = both_parts(grads_ref, slice(None))
+    for i in range(count):
+        keep = jnp.broadcast_to(limit_ref[:, :1], (outs, wide)) > first + i
+        s_real, s_imag = both_parts(spec_ref, pl.ds(step * count + i, 1))
+        real = jnp.where(keep, s_real * g_real + s_imag * g_imag, 0.0)
+        imag = jnp.where(keep, s_real * g_imag - s_imag * g_real, 0.0)
+        wgrad_ref[i, :, 0] = real.T.reshape(freqs, kx, outs)
+        wgrad_ref[i, :, 1] = imag.T.reshape(freqs, kx, outs)
     for c in range(block):
-        out_ref[c] = branch_of(lines[c], behind_ref[0]) + gain_ref[step * block + c] * grad_ref[c]
+        out_ref[c] = branch_of(lines[c], behind_ref[0]) + gain_ref[step * block + c] * grad_ref[step * block + c]
 
 
 def swap_groups(values, kx):
@@ -754,15 +768,12 @@
 
 
 def backward_kernel(
-    slabs, kx, part_ref, sums_ref, turned_ref, spec_ref, limit_ref, weight_ref,
-    out_ref, wgrad_ref, total_ref,
-    half_ref, give_ref, take_ref, g_buf, t_buf, grad_ref, back_ref, own_ref, near_ref, far_ref, pass_ref,
-    mode_a, slab_a, mode_b, slab_b, chan_sems, g_sems, t_sems, sum_mode, sum_slab,
+    slabs, kx, part_ref, sums_ref, turned_ref, weight_ref, out_ref, grad_ref, total_ref,
+    half_ref, give_ref, take_ref, t_buf, back_ref, own_ref, near_ref, far_ref, pass_ref,
+    mode_a, slab_a, mode_b, slab_b, chan_sems, t_sems, sum_mode, sum_slab,
 ):
-    ins, freqs = wgrad_ref.shape[0], wgrad_ref.shape[1]
-    outs = wgrad_ref.shape[4]
+    ins, outs, wide = turned_ref.shape[0], turned_ref.shape[1], turned_ref.shape[2] // 2
     mine_outs = outs // 2
-    wide = freqs * kx
     for i in range(ins):
         pltpu.make_async_copy(turned_ref.at[i], t_buf.at[i], t_sems.at[i]).start()
     greet(slabs)
@@ -802,26 +813,7 @@
     lax.fori_loop(0, ins, pull, 0)
     own_ref[...] = to_rows(back_ref, ins // 8, kx)
     state = gather_start(own_ref, out_ref, mode_b, slab_b, slabs)
-    share = ins // (slabs - 1)
-
-    def outer(i, carry):
-        keep = jnp.broadcast_to(limit_ref[:, :1], (outs, wide)) > first + i
-        g_real, g_imag = both_parts(grad_ref, slice(None))
-        s_real, s_imag = both_parts(spec_ref, pl.ds(i, 1))
-        real = jnp.where(keep, s_real * g_real + s_imag * g_imag, 0.0)
-        imag = jnp.where(keep, s_real * g_imag - s_imag * g_real, 0.0)
-        g_buf[i, :, 0] = real.T.reshape(freqs, kx, outs)
-        g_buf[i, :, 1] = imag.T.reshape(freqs, kx, outs)
-        pltpu.make_async_copy(g_buf.at[i], wgrad_ref.at[i], g_sems.at[i]).start()
-        return carry
-
-    done = [0]
-    def between(k):
-        stop = ins if k == 0 else done[0] + share
-        lax.fori_loop(done[0], stop, outer, 0)
-        done[0] = stop
-
-    gather_finish(state, out_ref, mode_b, slabs, between)
+    gather_finish(state, out_ref, mode_b, slabs, lambda k: None)
     total = pass_ref[...]
     for step, copy in zip(range(1, slabs), far):
         copy.wait()
@@ -831,11 +823,6 @@
     swap.wait_send()
     for wait in sent:
         wait()
-
-    def settle(i, carry):
-        pltpu.make_async_copy(g_buf.at[i], wgrad_ref.at[i], g_sems.at[i]).wait()
-        return carry
-    lax.fori_loop(0, ins, settle, 0)
 
 
 def fits(shapes, mesh_sizes):
@@ -877,7 +864,7 @@
     small = pl.BlockSpec((8, LANES), lambda g: (0, 0))
     field = jax.ShapeDtypeStruct(source_field.shape, jnp.float32)
     freq_field = jax.ShapeDtypeStruct((owners, groups, kx, LANES), jnp.float32)
-    params = pltpu.CompilerParams(dimension_semantics=("arbitrary",), vmem_limit_bytes=BIG)
+    params = pltpu.CompilerParams(dimension_semantics=("arbitrary",), vmem_limit_bytes=40 * 1024 * 1024)
     f32 = jnp.float32
 
     partial = pl.pallas_call(
@@ -907,7 +894,9 @@
     piece = (groups * kx, LANES)
     common = [vmem((slabs,) + piece, f32), vmem((slabs,) + piece, f32), vmem((slabs,) + piece, f32)]
     pair = [dma((2, slabs))] * 4
-    comm = lambda ident: pltpu.CompilerParams(collective_id=ident, has_side_effects=True, vmem_limit_bytes=BIG)
+    comm = lambda ident, room: pltpu.CompilerParams(
+        collective_id=ident, has_side_effects=True, vmem_limit_bytes=room * MIB
+    )
     gathered = jax.ShapeDtypeStruct((owners,) + piece, f32)
     flat = lambda lines: (2 * wide // LANES, lines, LANES)
     turned_shape = jax.ShapeDtypeStruct((channels, outs, 2 * wide), f32)
@@ -921,7 +910,7 @@
             vmem(weight.shape, f32), vmem(turned_shape.shape, f32), vmem(flat(outs), f32),
             vmem(flat(outs // 2), f32), vmem(piece, f32),
         ] + pair + [dma((2,)), dma((channels,)), dma((channels,))],
-        compiler_params=comm(20),
+        compiler_params=comm(20, 30),
         name="forward_modes",
     )(partial.reshape((owners,) + piece), weight, limit, weights)
 
@@ -932,8 +921,8 @@
             cells, cells, freq_cells, scalars, scalars, pick(ahead, "mode"), pick(row_ahead, "slab"),
             pick(row_behind, "slab"), pick(behind, "mode"),
         ],
-        out_specs=[cells, cells, freq_cells, small],
-        out_shape=[field, field, freq_field, jax.ShapeDtypeStruct((8, LANES), f32)],
+        out_specs=[cells, in_vmem, freq_cells, small],
+        out_shape=[field, pltpu.VMEM(field.shape, f32), freq_field, jax.ShapeDtypeStruct((8, LANES), f32)],
         scratch_shapes=[vmem((block * rows, 2 * cols), jnp.bfloat16)],
         compiler_params=params,
         name="middle",
@@ -942,30 +931,37 @@
         ahead, row_ahead, row_behind, behind,
     )
 
-    back_modes, weight_grad, totals = pl.pallas_call(
+    back_modes, all_grads, totals = pl.pallas_call(
         functools.partial(backward_kernel, slabs, kx),
-        in_specs=[in_vmem, in_vmem, anywhere, in_vmem, in_vmem, in_vmem],
-        out_specs=[in_vmem, anywhere, in_vmem],
-        out_shape=[gathered, jax.ShapeDtypeStruct(weight.shape, f32), jax.ShapeDtypeStruct((8, LANES), f32)],
+        in_specs=[in_vmem, in_vmem, anywhere, in_vmem],
+        out_specs=[in_vmem, in_vmem, in_vmem],
+        out_shape=[gathered, jax.ShapeDtypeStruct(flat(outs), f32), jax.ShapeDtypeStruct((8, LANES), f32)],
         scratch_shapes=common + [
-            vmem(weight.shape, f32), vmem(turned_shape.shape, f32), vmem(flat(outs), f32),
-            vmem(flat(channels), f32), vmem(piece, f32), vmem((8, LANES), f32),
+            vmem(turned_shape.shape, f32), vmem(flat(channels), f32), vmem(piece, f32), vmem((8, LANES), f32),
             vmem((slabs, 8, LANES), f32), vmem((8, LANES), f32),
-        ] + pair + [dma((2,)), dma((channels,)), dma((channels,)), dma((2,)), dma((2, slabs))],
-        compiler_params=comm(21),
+        ] + pair + [dma((2,)), dma((channels,)), dma((2,)), dma((2, slabs))],
+        compiler_params=comm(21, 16),
         name="backward_modes",
-    )(grad_partial.reshape((owners,) + piece), sums, turned, spec, limit, weights)
-    spectral_grad = weight_grad.transpose(0, 4, 1, 2, 3)
-
-    field_grad = pl.pallas_call(
-        functools.partial(last_packed, span),
+    )(grad_partial.reshape((owners,) + piece), sums, turned, weights)
+
+    count = channels // groups
+    whole = lambda array: pl.BlockSpec(array.shape, lambda g: (0,) * array.ndim)
+    field_grad, weight_grad = pl.pallas_call(
+        functools.partial(last_packed, span, kx),
         grid=(groups,),
-        in_specs=[cells, freq_cells, scalars, pick(row_behind, "slab"), pick(behind, "mode")],
-        out_specs=cells,
-        out_shape=field,
+        in_specs=[
+            in_vmem, freq_cells, scalars, pick(row_behind, "slab"), pick(behind, "mode"),
+            whole(all_grads), whole(spec), whole(limit),
+        ],
+        out_specs=[cells, pl.BlockSpec((count,) + weight.shape[1:], lambda g: (g, 0, 0, 0, 0))],
+        out_shape=[field, jax.ShapeDtypeStruct(weight.shape, f32)],
         compiler_params=params,
         name="last",
-    )(grad_sum, back_modes.reshape(freq_field.shape), skip_gain, row_behind, behind)
+    )(
+        pltpu.with_memory_space_constraint(grad_sum, pltpu.VMEM), back_modes.reshape(freq_field.shape), skip_gain,
+        row_behind, behind, all_grads, spec, limit,
+    )
+    spectral_grad = weight_grad.transpose(0, 4, 1, 2, 3)
     return (output, field_grad, spectral_grad, totals[0, :channels], totals[1, :channels])
 
 

time: 133 us -> 125 us (0.940)
  Pallas kernels: 119 us -> 115 us
  local copies, waits for them, and re-layouts: 12 us -> 8.75 us
    pallas_call x1, Pallas kernels: 16.7 us -> 12.1 us  [local(): pl.pallas_call(functools.partial(last_packed, span, kx), grid=(groups,),...]
    unnamed x5 -> x26, local copies, waits for them, and re-layouts: 9.03 us -> 7.04 us
    pallas_call x1, Pallas kernels: 28.9 us -> 30.5 us  [local(): pl.pallas_call(functools.partial(forward_kernel, slabs, kx), in_specs=[in...]
where the time goes in v2:
time: 125 us
  Pallas kernels  115 us (92%)
  local copies, waits for them, and re-layouts  8.75 us (7%)
    pallas_call x1, Pallas kernels, local(): pl.pallas_call(functools.partial(forward_kernel, slabs, kx), in_specs=[in...  30.5 us
    pallas_call x1, Pallas kernels, local(): pl.pallas_call(functools.partial(middle_packed, span), grid=(groups,), in...  30.4 us
    pallas_call x1, Pallas kernels, local(): pl.pallas_call(functools.partial(backward_kernel, slabs, kx), in_specs=[i...  28.9 us
    pallas_call x1, Pallas kernels, local(): pl.pallas_call(functools.partial(spectrum_packed, span), grid=(groups,),...  13.1 us
    pallas_call x1, Pallas kernels, local(): pl.pallas_call(functools.partial(last_packed, span, kx), grid=(groups,),...  12.1 us
    unnamed x26, local copies, waits for them, and re-layouts  7.04 us

profile of v2, /device:TPU:0, one launch (start us, length us, event | category | flops | bytes accessed | tf_op | source)
XLA Modules:
  0.0 124.6 jit_solution(17628609753410740071)
XLA Ops:
  0.6 0.0 copy-start
  0.7 0.7 copy-done
  1.3 0.1 constant_dynamic-slice_fusion
  1.4 0.1 tile.9
  1.5 0.1 broadcast_in_dim.32
  1.6 0.1 broadcast_in_dim.33
  1.6 0.0 slice-start
  1.7 0.1 and_select_fusion.weight_ref
  1.7 0.9 broadcast_in_dim.31.limit_ref
  2.6 0.0 copy-start.2
  2.6 1.4 %copy-done.2 = bf16[4,128,768]{2,1,0:T(8,128)(2,1)S(1)} copy-done((bf16[4,128,768]{2,1,0:T(8,128)(2,1)S(1)}, bf16[4,128,768]{2,1,0:T(8,128)(2,1)}, u32[]{:S(2)}) %copy-start.2) | copy-done | bytes 786456
  4.0 0.0 copy-start.3
  4.0 1.0 copy-done.3
  5.0 0.0 copy-start.7
  5.0 0.0 slice-start.1
  5.0 13.1 %spectrum.1 = f32[8,8,16,128]{3,2,1,0:T(8,128)S(1)} custom-call(f32[32,256,512]{2,1,0:T(8,128)} %x_ref.3, bf16[2,1024,128]{2,1,0:T(8,128)(2,1)S(1)} %copy-done.3, bf16[4,128,768]{2,1,0:T(8,128)(2,1)S(1)} %copy-done.2), custom_call_target="tpu_custom_call" | custom-call | tf_op jit(solution)/shard_map/spectrum/pallas_call | solution.py:870
  18.2 0.0 slice-done
  18.2 0.0 slice-done.1
  18.2 30.5 %forward_modes.1 = (f32[8,128,128]{2,1,0:T(8,128)S(1)}, f32[32,64,512]{2,1,0:T(8,128)S(1)}, f32[4,32,128]{2,1,0:T(8,128)S(1)}) custom-call(f32[8,128,128]{2,1,0:T(8,128)S(1)} %bitcast.17, f32[32,16,2,16,64]{4,3,2,1,0:T(8,128)S(1)} %bitcast.16, s32[64,128]{1,0:T(8,128)S(1)} %broadcast_in_dim.31.limit_ref, f32[2,32,128]{2,1,0:T(8,128)S(1)} %and_select_fusion.weight_ref), custom_call_target="tpu_custom_call" | custom-call | tf_op jit(solution)/shard_map/forward_modes/pallas_call | solution.py:904
  48.7 0.0 copy-start.4
  48.7 0.8 copy-done.4
  49.5 0.0 copy-start.9
  49.5 0.0 copy-start.1
  49.5 30.4 %middle.1 = (f32[32,256,512]{2,1,0:T(8,128)}, f32[32,256,512]{2,1,0:T(8,128)S(1)}, f32[8,8,16,128]{3,2,1,0:T(8,128)}, f32[8,128]{1,0:T(8,128)}) custom-call(f32[32,256,512]{2,1,0:T(8,128)} %x_ref.3, f32[32,256,512]{2,1,0:T(8,128)} %cot_ref.1, f32[8,8,16,128]{3,2,1,0:T(8,128)} %bitcast.18, f32[32]{0:T(128)} %gain_ref.3, f32[32]{0:T(128)} %bias_ref.1, ...), custom_call_target="tpu_custom_call" | custom-call | tf_op jit(solution)/shard_map/middle/pallas_call | solution.py:917
  79.8 0.0 copy-done.7
  79.8 0.0 copy-done.9
  79.9 0.0 copy-start.6
  79.9 1.0 copy-done.6
  80.9 0.0 copy-start.10
  80.9 0.7 copy-done.10
  81.6 28.9 %backward_modes.1 = (f32[8,128,128]{2,1,0:T(8,128)S(1)}, f32[4,64,128]{2,1,0:T(8,128)S(1)}, f32[8,128]{1,0:T(8,128)S(1)}) custom-call(f32[8,128,128]{2,1,0:T(8,128)S(1)} %bitcast.20, f32[8,128]{1,0:T(8,128)S(1)} %copy-done.10, f32[32,64,512]{2,1,0:T(8,128)S(1)} %get-tuple-element.22.turned_ref, f32[2,32,128]{2,1,0:T(8,128)S(1)} %and_select_fusion.weight_ref), custom_call_target="tpu_custom_call" | custom-call | tf_op jit(solution)/shard_map/backward_modes/pallas_call | solution.py:934
  110.5 0.0 copy-start.5
  110.5 0.8 copy-done.5
  111.3 0.0 copy-start.8
  111.3 0.6 copy-done.8
  112.0 0.5 slice_bitcast_fusion
  112.5 12.1 %last.1 = (f32[32,256,512]{2,1,0:T(8,128)}, f32[32,16,2,16,64]{4,3,2,1,0:T(8,128)}) custom-call(f32[32,256,512]{2,1,0:T(8,128)S(1)} %get-tuple-element.19.grad_ref, f32[8,8,16,128]{3,2,1,0:T(8,128)} %bitcast.19, f32[32]{0:T(128)} %gain_ref.3, bf16[4,256,384]{2,1,0:T(8,128)(2,1)} %constant.42.clone.row_back_ref, ...), custom_call_target="tpu_custom_call" | custom-call | tf_op jit(solution)/shard_map/last/pallas_call | solution.py:949
  124.6 0.0 copy-done.1
  (7 shorter events, 0.0 us)
Async XLA Ops:
  0.6 0.7 copy-start
  1.6 16.5 %slice-start = ((s8[8388608]{0:T(1024)(128)(4,1)}), s8[4194304]{0:T(1024)(128)(4,1)S(1)}, s32[]{:S(2)}) async-start(s8[8388608]{0:T(1024)(128)(4,1)} %bitcast.14), calls=%async_computation | async-start | bytes 8388608
  2.6 1.4 %copy-start.2 = (bf16[4,128,768]{2,1,0:T(8,128)(2,1)S(1)}, bf16[4,128,768]{2,1,0:T(8,128)(2,1)}, u32[]{:S(2)}) copy-start(bf16[4,128,768]{2,1,0:T(8,128)(2,1)} %constant.41.clone.row_ref) | copy-start | bytes 2359300
  4.0 1.0 copy-start.3
  5.0 74.8 %copy-start.7 = (s32[64,128]{1,0:T(8,128)}, s32[64,128]{1,0:T(8,128)S(1)}, u32[]{:S(2)}) copy-start(s32[64,128]{1,0:T(8,128)S(1)} %broadcast_in_dim.31.limit_ref) | copy-start | bytes 98308
  5.0 13.1 %slice-start.1 = ((s8[8388608]{0:T(1024)(128)(4,1)}), s8[4194304]{0:T(1024)(128)(4,1)S(1)}, s32[]{:S(2)}) async-start(s8[8388608]{0:T(1024)(128)(4,1)} %bitcast.14), calls=%async_computation.1 | async-start | bytes 8388608
  48.7 0.8 copy-start.4
  49.5 30.4 %copy-start.9 = (f32[4,32,128]{2,1,0:T(8,128)}, f32[4,32,128]{2,1,0:T(8,128)S(1)}, u32[]{:S(2)}) copy-start(f32[4,32,128]{2,1,0:T(8,128)S(1)} %get-tuple-element.25.spec_ref) | copy-start | bytes 196612
  49.5 75.1 %copy-start.1 = (s32[64,2]{0,1:T(2,128)S(1)}, s32[64,2]{0,1:T(2,128)}, u32[]{:S(2)}) copy-start(s32[64,2]{0,1:T(2,128)} %param.16) | copy-start | bytes 1540
  79.9 1.0 copy-start.6
  80.9 0.7 copy-start.10
  110.5 0.8 copy-start.5
  111.3 0.6 copy-start.8

commit v3 on v2

--- a/solution.py
+++ b/solution.py
@@ -13,6 +13,7 @@
 LANES = 128
 BIG = 60 * 1024 * 1024
 MIB = 1024 * 1024
+FORWARD, MIDDLE, LAST = 40, 40, 40
 
 
 def split_table(table):
@@ -423,18 +424,17 @@
     cols = parts.shape[1]
     high, low = halves_of(parts)
     ahead = np.stack([high, low], axis=3).reshape(modes, cols, -1)
-    ahead = np.concatenate([ahead, ahead], axis=1)
     flat_high = high.reshape(modes, cols, -1).transpose(0, 2, 1)
     flat_low = low.reshape(modes, cols, -1).transpose(0, 2, 1)
-    behind = np.concatenate([flat_high, flat_low, flat_high, flat_low], axis=1)
+    behind = np.concatenate([flat_high, flat_low], axis=1)
     wave = np.arange(kx_all)
     wave = wave + np.where(2 * wave >= kx_all, all_rows - kx_all, 0)
     angle = (np.arange(all_rows)[:, None] * wave[None, :] % all_rows) * (2.0 * np.pi / all_rows)
     table = np.concatenate([np.cos(angle), np.sin(angle)], axis=1).reshape(slabs, -1, 2 * kx_all)
     high, low = halves_of(table)
-    row_behind = np.concatenate([high, high, low], axis=2)
+    row_behind = np.concatenate([high, low], axis=2)
     high, low = high.transpose(0, 2, 1), low.transpose(0, 2, 1)
-    row_ahead = np.concatenate([high, low, high], axis=2)
+    row_ahead = np.concatenate([high, low], axis=2)
     return ahead, row_ahead, row_behind, behind
 
 
@@ -459,13 +459,26 @@
     return jnp.where(first, -back, ahead) if sign > 0 else jnp.where(first, back, -ahead)
 
 
-def mix_rows(lines, row_table, rows, span, out_ref, kx):
+def three_way(row_table, values):
+    high, low = high_low(values)
+    width = row_table.shape[1] // 2
+    left = jnp.concatenate([row_table, row_table[:, :width]], axis=1)
+    right = jnp.concatenate([high, high, low], axis=0)
+    return jnp.dot(left, right, preferred_element_type=jnp.float32)
+
+
+def two_way(values, table):
+    high, low = high_low(values)
+    both = jnp.concatenate([high, low], axis=1)
+    return jnp.dot(both, jnp.concatenate([table, table], axis=0), preferred_element_type=jnp.float32)
+
+
+def mix_rows(lines_ref, row_table, rows, span, kx, store):
     block = LANES // span
     mixed = []
     for c in range(0, block, 2):
-        pair = jnp.concatenate([lines[c * rows : (c + 1) * rows], lines[(c + 1) * rows : (c + 2) * rows]], axis=1)
-        high, low = high_low(pair)
-        both = jnp.dot(row_table, jnp.concatenate([high, high, low], axis=0), preferred_element_type=jnp.float32)
+        pair = [lines_ref[(c + k) * rows : (c + k + 1) * rows] for k in range(2)]
+        both = three_way(row_table, jnp.concatenate(pair, axis=1))
         mixed += [both[:, :LANES], both[:, LANES:]]
     lane = lanes_of(mixed[0].shape)
     pairs = []
@@ -483,14 +496,7 @@
     for m, values in enumerate(owners):
         done = values[:all_kx] + quarter_turn(values[all_kx:], span, -1)
         for s in range(slabs):
-            out_ref[m * slabs + s, 0] = done[s * kx : (s + 1) * kx]
-
-
-def spectrum_packed(span, x_ref, ahead_ref, row_ref, out_ref):
-    block, rows, cols = x_ref.shape
-    high, low = high_low(x_ref[...].reshape(block * rows, cols))
-    lines = jnp.dot(jnp.concatenate([high, low], axis=1), ahead_ref[0], preferred_element_type=jnp.float32)
-    mix_rows(lines, row_ref[0], rows, span, out_ref, out_ref.shape[2])
+            store(m * slabs + s, done[s * kx : (s + 1) * kx])
 
 
 def group_lines(modes_ref, row_table, span):
@@ -512,51 +518,71 @@
         sides.append(jnp.where(even, first, second))
     lines = []
     for c in range(0, block, 2):
-        high, low = high_low(jnp.concatenate([sides[c], sides[c + 1]], axis=1))
-        both = jnp.dot(row_table, jnp.concatenate([high, low, high], axis=0), preferred_element_type=jnp.float32)
+        both = three_way(row_table, jnp.concatenate([sides[c], sides[c + 1]], axis=1))
         lines += [both[:, :LANES], both[:, LANES:]]
     return lines
 
 
-def branch_of(lines, behind):
-    high, low = high_low(lines)
-    return jnp.dot(jnp.concatenate([high, low], axis=1), behind, preferred_element_type=jnp.float32)
-
-
 def middle_packed(
     span, x_ref, cot_ref, modes_ref, gain_ref, bias_ref, ahead_ref, row_ref, row_back_ref, behind_ref,
-    out_ref, grad_ref, spec_ref, sums_ref, split_ref,
+    out_ref, grad_ref, spec_ref, sums_ref, split_ref, lines_ref,
 ):
-    block, rows, cols = x_ref.shape
+    block, rows, cols = cot_ref.shape
+    kx = modes_ref.shape[2]
     step = pl.program_id(0)
     scale = math.sqrt(2.0 / math.pi)
+    row_table = row_ref[0]
 
     @pl.when(step == 0)
     def _():
         sums_ref[...] = jnp.zeros_like(sums_ref)
 
-    lines = group_lines(modes_ref, row_back_ref[0], span)
+    def ahead(c):
+        here = slice(c * rows, (c + 1) * rows)
+        both = jnp.concatenate([ahead_ref[0], ahead_ref[0]], axis=0)
+        lines_ref[here] = jnp.dot(split_ref[here], both, preferred_element_type=jnp.float32)
+
+    def finish(group):
+        def store(owner, values):
+            spec_ref[owner, pl.ds(pl.multiple_of(group * kx, kx), kx)] = values
+        mix_rows(lines_ref, row_table, rows, span, kx, store)
+
     lane = lanes_of(sums_ref.shape)
     line = lax.broadcasted_iota(jnp.int32, sums_ref.shape, 0)
-    for c in range(block):
-        source = x_ref[c]
-        v = branch_of(lines[c], behind_ref[0]) + (gain_ref[step * block + c] * source + bias_ref[step * block + c])
+
+    def cell(c, lines):
+        channel = step * block + c
+        source = x_ref[channel]
+        v = two_way(lines, behind_ref[0]) + (gain_ref[channel] * source + bias_ref[channel])
         square = v * v
         inner = v * (scale + (scale * 0.044715) * square)
         up = 0.5 + 0.5 * jnp.tanh(inner)
         out_ref[c] = v * up
         bend = v * (2.0 * scale + (6.0 * scale * 0.044715) * square)
         grad = cot_ref[c] * (up + (up * (1.0 - up)) * bend)
-        grad_ref[step * block + c] = grad
+        grad_ref[channel] = grad
         high, low = high_low(grad)
         split_ref[c * rows : (c + 1) * rows, :cols] = high
         split_ref[c * rows : (c + 1) * rows, cols:] = low
         gate = jnp.sum(jnp.sum(grad * source, axis=0, keepdims=True), axis=1, keepdims=True)
         bias = jnp.sum(jnp.sum(grad, axis=0, keepdims=True), axis=1, keepdims=True)
-        here = (lane == step * block + c) & (line < 2)
+        here = (lane == channel) & (line < 2)
         sums_ref[...] = jnp.where(here, jnp.where(line == 0, gate, bias), sums_ref[...])
-    made = jnp.dot(split_ref[...], ahead_ref[0], preferred_element_type=jnp.float32)
-    mix_rows(made, row_ref[0], rows, span, spec_ref, spec_ref.shape[2])
+
+    for c in range(block):
+        ahead(c)
+    lines = group_lines(modes_ref, row_back_ref[0], span)
+    for c in range(block // 2):
+        cell(c, lines[c])
+    finish(jnp.maximum(step - 1, 0))
+    for c in range(block // 2, block):
+        cell(c, lines[c])
+
+    @pl.when(step == pl.num_programs(0) - 1)
+    def _():
+        for c in range(block):
+            ahead(c)
+        finish(step)
 
 
 def last_packed(
@@ -577,7 +603,7 @@
         wgrad_ref[i, :, 0] = real.T.reshape(freqs, kx, outs)
         wgrad_ref[i, :, 1] = imag.T.reshape(freqs, kx, outs)
     for c in range(block):
-        out_ref[c] = branch_of(lines[c], behind_ref[0]) + gain_ref[step * block + c] * grad_ref[step * block + c]
+        out_ref[c] = two_way(lines[c], behind_ref[0]) + gain_ref[step * block + c] * grad_ref[step * block + c]
 
 
 def swap_groups(values, kx):
@@ -710,31 +736,124 @@
 
 
 def forward_kernel(
-    slabs, kx, part_ref, w_ref, limit_ref, weight_ref, out_ref, turned_ref, spec_ref,
-    half_ref, give_ref, take_ref, w_buf, t_buf, sum_ref, peer_ref, own_ref,
-    mode_a, slab_a, mode_b, slab_b, chan_sems, w_sems, t_sems,
+    span, slabs, kx, x_ref, ahead_ref, row_ref, w_ref, limit_ref, weight_ref, out_ref, turned_ref, spec_ref, x_buf,
+    part_ref, half_ref, give_ref, take_ref, w_buf, t_buf, sum_ref, peer_ref, own_ref, lines_ref, ahead_buf, row_buf,
+    mode_a, slab_a, mode_b, slab_b, chan_sems, x_sems, w_sems, table_sems, t_sems,
 ):
-    ins, freqs = w_ref.shape[0], w_ref.shape[1]
-    outs = w_ref.shape[4]
+    ins, freqs, outs = w_ref.shape[0], w_ref.shape[1], w_ref.shape[4]
+    rows, cols = x_ref.shape[1:]
+    block = LANES // span
+    groups = ins // block
     mine_outs = outs // 2
     wide = freqs * kx
-    for i in range(ins):
-        pltpu.make_async_copy(w_ref.at[i], w_buf.at[i], w_sems.at[i]).start()
+    me_mode, me_slab = lax.axis_index("mode"), lax.axis_index("slab")
+    peer_mode = other("mode", 1, 2)
+    first = lax.axis_index("chan") * ins
+    tables = [
+        pltpu.make_async_copy(ahead_ref.at[me_mode], ahead_buf, table_sems.at[0]),
+        pltpu.make_async_copy(row_ref.at[me_slab], row_buf, table_sems.at[1]),
+    ]
+    tables[0].start()
+
+    def x_copy(k):
+        here = pl.ds(k * (block // 2), block // 2)
+        return pltpu.make_async_copy(x_ref.at[here], x_buf.at[here], x_sems.at[k])
+
+    def w_copy(g):
+        here = pl.ds(g * block, block)
+        return pltpu.make_async_copy(w_ref.at[here], w_buf.at[here], w_sems.at[g])
+
+    for g in range(groups):
+        x_copy(2 * g).start()
+        x_copy(2 * g + 1).start()
+        if g == 0:
+            tables[1].start()
+        if g > 0:
+            w_copy(g - 1).start()
+    w_copy(groups - 1).start()
     greet(slabs)
-    first = lax.axis_index("chan") * ins
-
-    def flip():
-        def body(i, carry):
-            pltpu.make_async_copy(w_ref.at[i], w_buf.at[i], w_sems.at[i]).wait()
+
+    def t_copy(g):
+        here = pl.ds(g * block, block)
+        return pltpu.make_async_copy(t_buf.at[here], turned_ref.at[here], t_sems.at[g])
+
+    def place(g):
+        return pl.ds(pl.multiple_of(g * kx, kx), kx)
+
+    def mode_copy(g):
+        return pltpu.make_async_remote_copy(
+            src_ref=part_ref.at[pl.ds(peer_mode * slabs, slabs), place(g)], dst_ref=half_ref.at[:, place(g)],
+            send_sem=mode_a.at[0, g], recv_sem=mode_a.at[1, g],
+            device_id={"mode": peer_mode}, device_id_type=pl.DeviceIdType.MESH,
+        )
+
+    def slab_copy(step, g):
+        return pltpu.make_async_remote_copy(
+            src_ref=give_ref.at[step, place(g)], dst_ref=take_ref.at[step, place(g)],
+            send_sem=slab_a.at[0, step, g], recv_sem=slab_a.at[1, step, g],
+            device_id={"slab": other("slab", step, slabs)}, device_id_type=pl.DeviceIdType.MESH,
+        )
+
+    def ahead(g):
+        x_copy(2 * g).wait()
+        x_copy(2 * g + 1).wait()
+        values = x_buf[pl.ds(g * block, block)].reshape(block * rows, cols)
+        lines_ref[...] = two_way(values, ahead_buf[...])
+
+    def finish(g):
+        def store(owner, values):
+            part_ref[owner, place(g)] = values
+        mix_rows(lines_ref, row_buf[...], rows, span, kx, store)
+
+    def flip(g):
+        for k in range(block):
+            i = g * block + k
             keep = jnp.broadcast_to(limit_ref[:, :1], (outs, wide)) > first + i
             for p in range(2):
                 turned = w_buf[i, :, p].reshape(wide, outs).T
                 t_buf[i, :, p * wide : (p + 1) * wide] = jnp.where(keep, turned, 0.0)
-            pltpu.make_async_copy(t_buf.at[i], turned_ref.at[i], t_sems.at[i]).start()
-            return carry
-        lax.fori_loop(0, ins, body, 0)
-
-    mine, sent = scatter_sum(part_ref, half_ref, give_ref, take_ref, mode_a, slab_a, slabs, flip)
+
+    def pass_on(g):
+        mode_copy(g).wait_recv()
+        for step in [slabs // 2] + [step for step in range(1, slabs) if step != slabs // 2]:
+            slab = other("slab", step, slabs)
+            give_ref[step, place(g)] = part_ref[me_mode * slabs + slab, place(g)] + half_ref[slab, place(g)]
+            slab_copy(step, g).start()
+
+    for table in tables:
+        table.wait()
+    ahead(0)
+
+    def body(g, carry):
+        w_copy(g - 1).wait()
+        finish(g - 1)
+        flip(g - 1)
+        ahead(g)
+        t_copy(g - 1).start()
+        mode_copy(g - 1).start()
+
+        @pl.when(g > 1)
+        def _():
+            pass_on(g - 2)
+        return carry
+
+    lax.fori_loop(1, groups, body, 0)
+    w_copy(groups - 1).wait()
+    finish(groups - 1)
+    mode_copy(groups - 1).start()
+    pass_on(groups - 2)
+    flip(groups - 1)
+    t_copy(groups - 1).start()
+    pass_on(groups - 1)
+    mine = part_ref[me_mode * slabs + me_slab] + half_ref[me_slab]
+
+    def landed(g, carry):
+        for step in range(1, slabs):
+            slab_copy(step, g).wait_recv()
+        return carry
+    lax.fori_loop(0, groups, landed, 0)
+    for step in range(1, slabs):
+        mine = mine + take_ref[step]
     to_lanes(mine, spec_ref, kx)
 
     def contract(i, carry):
@@ -758,24 +877,25 @@
     state = gather_start(own_ref, out_ref, mode_b, slab_b, slabs)
     gather_finish(state, out_ref, mode_b, slabs, lambda k: None)
     swap.wait_send()
-    for wait in sent:
-        wait()
-
-    def settle(i, carry):
-        pltpu.make_async_copy(t_buf.at[i], turned_ref.at[i], t_sems.at[i]).wait()
+
+    def settle(g, carry):
+        t_copy(g).wait()
+        mode_copy(g).wait_send()
+        for step in range(1, slabs):
+            slab_copy(step, g).wait_send()
         return carry
-    lax.fori_loop(0, ins, settle, 0)
+    lax.fori_loop(0, groups, settle, 0)
 
 
 def backward_kernel(
     slabs, kx, part_ref, sums_ref, turned_ref, weight_ref, out_ref, grad_ref, total_ref,
     half_ref, give_ref, take_ref, t_buf, back_ref, own_ref, near_ref, far_ref, pass_ref,
-    mode_a, slab_a, mode_b, slab_b, chan_sems, t_sems, sum_mode, sum_slab,
+    mode_a, slab_a, mode_b, slab_b, chan_sems, sum_mode, sum_slab, t_sem,
 ):
-    ins, outs, wide = turned_ref.shape[0], turned_ref.shape[1], turned_ref.shape[2] // 2
+    ins, outs, wide = t_buf.shape[0], t_buf.shape[1], t_buf.shape[2] // 2
     mine_outs = outs // 2
-    for i in range(ins):
-        pltpu.make_async_copy(turned_ref.at[i], t_buf.at[i], t_sems.at[i]).start()
+    load = pltpu.make_async_copy(turned_ref, t_buf, t_sem)
+    load.start()
     greet(slabs)
     first = lax.axis_index("chan") * ins
     near = send(sums_ref, near_ref, sum_mode.at[0], sum_mode.at[1], "mode", other("mode", 1, 2))
@@ -797,11 +917,7 @@
     swap = send(
         grad_ref.at[:, here], grad_ref.at[:, here], chan_sems.at[0], chan_sems.at[1], "chan", other("chan", 1, 2)
     )
-
-    def arrive(i, carry):
-        pltpu.make_async_copy(turned_ref.at[i], t_buf.at[i], t_sems.at[i]).wait()
-        return carry
-    lax.fori_loop(0, ins, arrive, 0)
+    load.wait()
     swap.wait_recv()
 
     def pull(i, carry):
@@ -861,21 +977,10 @@
     cells = pl.BlockSpec((block, rows, cols), lambda g: (g, 0, 0))
     freq_cells = pl.BlockSpec((owners, 1, kx, LANES), lambda g: (0, g, 0, 0))
     scalars = pl.BlockSpec(memory_space=pltpu.SMEM)
-    small = pl.BlockSpec((8, LANES), lambda g: (0, 0))
     field = jax.ShapeDtypeStruct(source_field.shape, jnp.float32)
     freq_field = jax.ShapeDtypeStruct((owners, groups, kx, LANES), jnp.float32)
-    params = pltpu.CompilerParams(dimension_semantics=("arbitrary",), vmem_limit_bytes=40 * 1024 * 1024)
+    room = lambda size: pltpu.CompilerParams(dimension_semantics=("arbitrary",), vmem_limit_bytes=size * MIB)
     f32 = jnp.float32
-
-    partial = pl.pallas_call(
-        functools.partial(spectrum_packed, span),
-        grid=(groups,),
-        in_specs=[cells, pick(ahead, "mode"), pick(row_ahead, "slab")],
-        out_specs=freq_cells,
-        out_shape=freq_field,
-        compiler_params=params,
-        name="spectrum",
-    )(source_field, ahead, row_ahead)
 
     weight = spectral_weight.transpose(0, 2, 3, 4, 1)
     col_freq = mode_index * freqs + jnp.arange(freqs, dtype=jnp.int32)
@@ -897,52 +1002,59 @@
     comm = lambda ident, room: pltpu.CompilerParams(
         collective_id=ident, has_side_effects=True, vmem_limit_bytes=room * MIB
     )
-    gathered = jax.ShapeDtypeStruct((owners,) + piece, f32)
     flat = lambda lines: (2 * wide // LANES, lines, LANES)
-    turned_shape = jax.ShapeDtypeStruct((channels, outs, 2 * wide), f32)
-
-    out_modes, turned, spec = pl.pallas_call(
-        functools.partial(forward_kernel, slabs, kx),
-        in_specs=[in_vmem, anywhere, in_vmem, in_vmem],
-        out_specs=[in_vmem, anywhere, in_vmem],
-        out_shape=[gathered, turned_shape, jax.ShapeDtypeStruct(flat(channels), f32)],
-        scratch_shapes=common + [
-            vmem(weight.shape, f32), vmem(turned_shape.shape, f32), vmem(flat(outs), f32),
-            vmem(flat(outs // 2), f32), vmem(piece, f32),
-        ] + pair + [dma((2,)), dma((channels,)), dma((channels,))],
-        compiler_params=comm(20, 30),
+
+    in_hbm = lambda array: pltpu.with_memory_space_constraint(array, pltpu.HBM)
+    held = lambda array: pltpu.with_memory_space_constraint(array, pltpu.VMEM)
+    modes_shape = (owners,) + piece
+    out_modes, turned, spec, source_held = pl.pallas_call(
+        functools.partial(forward_kernel, span, slabs, kx),
+        in_specs=[anywhere, anywhere, anywhere, anywhere, in_vmem, in_vmem],
+        out_specs=[in_vmem, anywhere, in_vmem, in_vmem],
+        out_shape=[
+            jax.ShapeDtypeStruct(modes_shape, f32), pltpu.HBM((channels, outs, 2 * wide), f32),
+            jax.ShapeDtypeStruct(flat(channels), f32), pltpu.VMEM(field.shape, f32),
+        ],
+        scratch_shapes=[vmem(modes_shape, f32)] + common + [
+            vmem(weight.shape, f32), vmem((channels, outs, 2 * wide), f32), vmem(flat(outs), f32), vmem(flat(outs // 2), f32), vmem(piece, f32),
+            vmem((block * rows, LANES), f32), vmem(ahead.shape[1:], jnp.bfloat16), vmem(row_ahead.shape[1:], jnp.bfloat16),
+            dma((2, groups)), dma((2, slabs, groups)), dma((2, slabs)), dma((2, slabs)), dma((2,)),
+            dma((2 * groups,)), dma((groups,)), dma((2,)), dma((groups,)),
+        ],
+        compiler_params=comm(20, FORWARD),
         name="forward_modes",
-    )(partial.reshape((owners,) + piece), weight, limit, weights)
+    )(in_hbm(source_field), in_hbm(ahead), in_hbm(row_ahead), in_hbm(weight), limit, weights)
 
     output, grad_sum, grad_partial, sums = pl.pallas_call(
         functools.partial(middle_packed, span),
         grid=(groups,),
         in_specs=[
-            cells, cells, freq_cells, scalars, scalars, pick(ahead, "mode"), pick(row_ahead, "slab"),
+            in_vmem, cells, freq_cells, scalars, scalars, pick(ahead, "mode"), pick(row_ahead, "slab"),
             pick(row_behind, "slab"), pick(behind, "mode"),
         ],
-        out_specs=[cells, in_vmem, freq_cells, small],
-        out_shape=[field, pltpu.VMEM(field.shape, f32), freq_field, jax.ShapeDtypeStruct((8, LANES), f32)],
-        scratch_shapes=[vmem((block * rows, 2 * cols), jnp.bfloat16)],
-        compiler_params=params,
+        out_specs=[cells, in_vmem, in_vmem, in_vmem],
+        out_shape=[field, pltpu.VMEM(field.shape, f32), jax.ShapeDtypeStruct(modes_shape, f32), jax.ShapeDtypeStruct((8, LANES), f32)],
+        scratch_shapes=[vmem((block * rows, 2 * cols), jnp.bfloat16), vmem((block * rows, LANES), f32)],
+        input_output_aliases={0: 1},
+        compiler_params=room(MIDDLE),
         name="middle",
     )(
-        source_field, cotangent, out_modes.reshape(freq_field.shape), skip_gain, channel_bias,
+        held(source_held), cotangent, out_modes.reshape(freq_field.shape), skip_gain, channel_bias,
         ahead, row_ahead, row_behind, behind,
     )
 
     back_modes, all_grads, totals = pl.pallas_call(
         functools.partial(backward_kernel, slabs, kx),
         in_specs=[in_vmem, in_vmem, anywhere, in_vmem],
-        out_specs=[in_vmem, in_vmem, in_vmem],
-        out_shape=[gathered, jax.ShapeDtypeStruct(flat(outs), f32), jax.ShapeDtypeStruct((8, LANES), f32)],
+        out_specs=[in_vmem] * 3,
+        out_shape=[jax.ShapeDtypeStruct(modes_shape, f32), jax.ShapeDtypeStruct(flat(outs), f32), jax.ShapeDtypeStruct((8, LANES), f32)],
         scratch_shapes=common + [
-            vmem(turned_shape.shape, f32), vmem(flat(channels), f32), vmem(piece, f32), vmem((8, LANES), f32),
+            vmem((channels, outs, 2 * wide), f32), vmem(flat(channels), f32), vmem(piece, f32), vmem((8, LANES), f32),
             vmem((slabs, 8, LANES), f32), vmem((8, LANES), f32),
-        ] + pair + [dma((2,)), dma((channels,)), dma((2,)), dma((2, slabs))],
-        compiler_params=comm(21, 16),
+        ] + pair + [dma((2,)), dma((2,)), dma((2, slabs)), dma],
+        compiler_params=comm(21, 20),
         name="backward_modes",
-    )(grad_partial.reshape((owners,) + piece), sums, turned, weights)
+    )(grad_partial, sums, in_hbm(turned), weights)
 
     count = channels // groups
     whole = lambda array: pl.BlockSpec(array.shape, lambda g: (0,) * array.ndim)
@@ -955,7 +1067,7 @@
         ],
         out_specs=[cells, pl.BlockSpec((count,) + weight.shape[1:], lambda g: (g, 0, 0, 0, 0))],
         out_shape=[field, jax.ShapeDtypeStruct(weight.shape, f32)],
-        compiler_params=params,
+        compiler_params=room(LAST),
         name="last",
     )(
         pltpu.with_memory_space_constraint(grad_sum, pltpu.VMEM), back_modes.reshape(freq_field.shape), skip_gain,

time: 125 us -> 114 us (0.912)
  Pallas kernels: 115 us -> 107 us
  local copies, waits for them, and re-layouts: 8.75 us -> 6 us
    pallas_call x1, Pallas kernels: 28.9 us -> 23.6 us  [local(): pl.pallas_call(functools.partial(backward_kernel, slabs, kx), in_specs=[i...]
    unnamed x26 -> x14, local copies, waits for them, and re-layouts: 7.04 us -> 3.83 us
    pallas_call x2 -> x1, Pallas kernels: 43.6 us -> 41.8 us  [local(): pl.pallas_call(functools.partial(forward_kernel, span, slabs, kx), in_spe...]
    pallas_call x1, Pallas kernels: 30.4 us -> 29.1 us  [local(): pl.pallas_call(functools.partial(middle_packed, span), grid=(groups,), in...]
where the time goes in v3:
time: 114 us
  Pallas kernels  107 us (94%)
  local copies, waits for them, and re-layouts  6 us (5%)
    pallas_call x1, Pallas kernels, local(): pl.pallas_call(functools.partial(forward_kernel, span, slabs, kx), in_spe...  41.8 us
    pallas_call x1, Pallas kernels, local(): pl.pallas_call(functools.partial(middle_packed, span), grid=(groups,), in...  29.1 us
    pallas_call x1, Pallas kernels, local(): pl.pallas_call(functools.partial(backward_kernel, slabs, kx), in_specs=[i...  23.6 us
    pallas_call x1, Pallas kernels, local(): pl.pallas_call(functools.partial(last_packed, span, kx), grid=(groups,),...  12.1 us
    unnamed x14, local copies, waits for them, and re-layouts  3.83 us

profile of v3, /device:TPU:0, one launch (start us, length us, event | category | flops | bytes accessed | tf_op | source)
XLA Modules:
  0.0 114.0 jit_solution(13220757158291180378)
XLA Ops:
  0.6 0.0 copy-start
  0.7 0.7 copy-done
  1.3 0.1 constant_dynamic-slice_fusion
  1.4 0.1 tile.9
  1.5 0.1 broadcast_in_dim.32
  1.6 0.1 broadcast_in_dim.33
  1.7 0.7 and_select_fusion.weight_ref
  2.4 1.3 %broadcast_in_dim.31.limit_ref = s32[64,128]{1,0:T(8,128)} broadcast(s32[64]{0:T(128)} %param.17), dimensions={0} | broadcast | bytes 33024 | tf_op jit(solution)/shard_map/broadcast_in_dim | solution.py:995
  3.7 41.8 %forward_modes.1 = (f32[8,128,128]{2,1,0:T(8,128)}, f32[32,64,512]{2,1,0:T(8,128)}, f32[4,32,128]{2,1,0:T(8,128)}, f32[32,256,512]{2,1,0:T(8,128)S(1)}) custom-call(f32[32,256,512]{2,1,0:T(8,128)} %x_ref.1, bf16[2,512,128]{2,1,0:T(8,128)(2,1)} %constant.40.clone.ahead_ref, bf16[4,128,512]{2,1,0:T(8,128)(2,1)} %constant.41.clone.row_ref, ...), custom_call_target="tpu_custom_call" | custom-call | tf_op jit(solution)/shard_map/forward_modes/pallas_call | solution.py:1010
  45.5 0.0 copy-start.4
  45.5 0.0 copy-start.1
  45.5 29.1 %middle.1 = (f32[32,256,512]{2,1,0:T(8,128)}, f32[32,256,512]{2,1,0:T(8,128)S(1)}, f32[8,128,128]{2,1,0:T(8,128)}, f32[8,128]{1,0:T(8,128)}) custom-call(f32[32,256,512]{2,1,0:T(8,128)S(1)} %get-tuple-element.18.x_ref, f32[32,256,512]{2,1,0:T(8,128)} %cot_ref.1, f32[8,8,16,128]{3,2,1,0:T(8,128)} %bitcast.14, ...), custom_call_target="tpu_custom_call", output_to_operand_aliasing={{1}: (0, {})} | custom-call | tf_op jit(solution)/shard_map/middle/pallas_call | solution.py:1028
  74.6 0.0 copy-done.4
  74.6 0.0 copy-start.2
  74.6 1.0 copy-done.2
  75.6 0.0 copy-start.6
  75.6 0.7 copy-done.6
  76.3 23.6 %backward_modes.1 = (f32[8,128,128]{2,1,0:T(8,128)S(1)}, f32[4,64,128]{2,1,0:T(8,128)S(1)}, f32[8,128]{1,0:T(8,128)S(1)}) custom-call(f32[8,128,128]{2,1,0:T(8,128)S(1)} %copy-done.2, f32[8,128]{1,0:T(8,128)S(1)} %copy-done.6, f32[32,64,512]{2,1,0:T(8,128)} %get-tuple-element.24.turned_ref, f32[2,32,128]{2,1,0:T(8,128)S(1)} %copy-done.4), custom_call_target="tpu_custom_call" | custom-call | tf_op jit(solution)/shard_map/backward_modes/pallas_call | solution.py:1046
  99.9 0.0 copy-start.3
  99.9 0.8 copy-done.3
  100.7 0.0 copy-start.5
  100.7 0.6 copy-done.5
  101.4 0.5 slice_bitcast_fusion
  101.9 12.1 %last.1 = (f32[32,256,512]{2,1,0:T(8,128)}, f32[32,16,2,16,64]{4,3,2,1,0:T(8,128)}) custom-call(f32[32,256,512]{2,1,0:T(8,128)S(1)} %get-tuple-element.21.grad_ref, f32[8,8,16,128]{3,2,1,0:T(8,128)} %bitcast.12, f32[32]{0:T(128)} %gain_ref.3, bf16[4,256,256]{2,1,0:T(8,128)(2,1)} %constant.42.clone.row_back_ref, ...), custom_call_target="tpu_custom_call" | custom-call | tf_op jit(solution)/shard_map/last/pallas_call | solution.py:1061
  114.0 0.0 copy-done.1
  (6 shorter events, 0.0 us)
Async XLA Ops:
  0.6 0.7 copy-start
  45.5 29.1 %copy-start.4 = (f32[2,32,128]{2,1,0:T(8,128)S(1)}, f32[2,32,128]{2,1,0:T(8,128)}, u32[]{:S(2)}) copy-start(f32[2,32,128]{2,1,0:T(8,128)} %and_select_fusion.weight_ref) | copy-start | bytes 98308
  45.5 68.5 %copy-start.1 = (s32[64,2]{0,1:T(2,128)S(1)}, s32[64,2]{0,1:T(2,128)}, u32[]{:S(2)}) copy-start(s32[64,2]{0,1:T(2,128)} %param.16) | copy-start | bytes 1540
  74.6 1.0 copy-start.2
  75.6 0.7 copy-start.6
  99.9 0.8 copy-start.3
  100.7 0.7 copy-start.5

commit v4 on v3

--- a/solution.py
+++ b/solution.py
@@ -13,7 +13,7 @@
 LANES = 128
 BIG = 60 * 1024 * 1024
 MIB = 1024 * 1024
-FORWARD, MIDDLE, LAST = 40, 40, 40
+FORWARD, MIDDLE, LAST, BACKWARD = 40, 40, 40, 20
 
 
 def split_table(table):
@@ -499,13 +499,14 @@
             store(m * slabs + s, done[s * kx : (s + 1) * kx])
 
 
-def group_lines(modes_ref, row_table, span):
+def group_lines(modes_ref, group, kx, row_table, span):
     block = LANES // span
     owners = modes_ref.shape[0]
     half = owners // 2
+    here = pl.ds(pl.multiple_of(group * kx, kx), kx)
     stack = []
     for m in range(2):
-        stack.append(jnp.concatenate([modes_ref[m * half + s, 0] for s in range(half)], axis=0))
+        stack.append(jnp.concatenate([modes_ref[m * half + s, here] for s in range(half)], axis=0))
     full = [jnp.concatenate([one, quarter_turn(one, span, 1)], axis=0) for one in stack]
     rolled = [[lane_roll(one, k * span) for k in range(block)] for one in full]
     lane = lanes_of(full[0].shape)
@@ -524,11 +525,10 @@
 
 
 def middle_packed(
-    span, x_ref, cot_ref, modes_ref, gain_ref, bias_ref, ahead_ref, row_ref, row_back_ref, behind_ref,
-    out_ref, grad_ref, spec_ref, sums_ref, split_ref, lines_ref,
+    span, kx, x_ref, cot_ref, modes_ref, gain_ref, bias_ref, ahead_ref, row_ref, row_back_ref, behind_ref,
+    out_ref, grad_ref, spec_ref, sums_ref, split_ref, lines_ref, branch_ref, next_ref, held_ref, made_ref,
 ):
     block, rows, cols = cot_ref.shape
-    kx = modes_ref.shape[2]
     step = pl.program_id(0)
     scale = math.sqrt(2.0 / math.pi)
     row_table = row_ref[0]
@@ -538,51 +538,73 @@
         sums_ref[...] = jnp.zeros_like(sums_ref)
 
     def ahead(c):
-        here = slice(c * rows, (c + 1) * rows)
-        both = jnp.concatenate([ahead_ref[0], ahead_ref[0]], axis=0)
-        lines_ref[here] = jnp.dot(split_ref[here], both, preferred_element_type=jnp.float32)
-
-    def finish(group):
+        here = slice(c * rows, (c + 2) * rows)
+        table = ahead_ref[0]
+        high = jnp.dot(split_ref[here, :cols], table, preferred_element_type=jnp.float32)
+        lines_ref[here] = high + jnp.dot(split_ref[here, cols:], table, preferred_element_type=jnp.float32)
+
+    def finish(from_ref, group):
         def store(owner, values):
             spec_ref[owner, pl.ds(pl.multiple_of(group * kx, kx), kx)] = values
-        mix_rows(lines_ref, row_table, rows, span, kx, store)
+        mix_rows(from_ref, row_table, rows, span, kx, store)
 
     lane = lanes_of(sums_ref.shape)
     line = lax.broadcasted_iota(jnp.int32, sums_ref.shape, 0)
 
     def cell(c, lines):
         channel = step * block + c
-        source = x_ref[channel]
-        v = two_way(lines, behind_ref[0]) + (gain_ref[channel] * source + bias_ref[channel])
-        square = v * v
-        inner = v * (scale + (scale * 0.044715) * square)
-        up = 0.5 + 0.5 * jnp.tanh(inner)
-        out_ref[c] = v * up
-        bend = v * (2.0 * scale + (6.0 * scale * 0.044715) * square)
-        grad = cot_ref[c] * (up + (up * (1.0 - up)) * bend)
-        grad_ref[channel] = grad
-        high, low = high_low(grad)
-        split_ref[c * rows : (c + 1) * rows, :cols] = high
-        split_ref[c * rows : (c + 1) * rows, cols:] = low
-        gate = jnp.sum(jnp.sum(grad * source, axis=0, keepdims=True), axis=1, keepdims=True)
-        bias = jnp.sum(jnp.sum(grad, axis=0, keepdims=True), axis=1, keepdims=True)
+        gain, shift = gain_ref[channel], bias_ref[channel]
+        branch_ref[c] = two_way(lines, behind_ref[0])
+        gate = jnp.zeros((8, cols), jnp.float32)
+        bias = jnp.zeros((8, cols), jnp.float32)
+        for r in range(0, rows, 16):
+            here = slice(r, r + 16)
+            source = x_ref[channel, here]
+            v = branch_ref[c, here] + (gain * source + shift)
+            square = v * v
+            inner = v * (scale + (scale * 0.044715) * square)
+            up = 0.5 + 0.5 * jnp.tanh(inner)
+            out_ref[c, here] = v * up
+            bend = v * (2.0 * scale + (6.0 * scale * 0.044715) * square)
+            grad = cot_ref[c, here] * (up + (up * (1.0 - up)) * bend)
+            grad_ref[channel, here] = grad
+            high, low = high_low(grad)
+            there = slice(c * rows + r, c * rows + r + 16)
+            split_ref[there, :cols] = high
+            split_ref[there, cols:] = low
+            both = grad * source
+            gate = gate + (both[:8] + both[8:])
+            bias = bias + (grad[:8] + grad[8:])
+        gate = jnp.sum(jnp.sum(gate, axis=0, keepdims=True), axis=1, keepdims=True)
+        bias = jnp.sum(jnp.sum(bias, axis=0, keepdims=True), axis=1, keepdims=True)
         here = (lane == channel) & (line < 2)
         sums_ref[...] = jnp.where(here, jnp.where(line == 0, gate, bias), sums_ref[...])
 
+    def prepare(group):
+        for c, lines in enumerate(group_lines(modes_ref, group, kx, row_back_ref[0], span)):
+            next_ref[c] = lines
+
+    @pl.when(step == 0)
+    def _():
+        prepare(0)
+
+    held_ref[...] = next_ref[...]
+    made_ref[...] = lines_ref[...]
     for c in range(block):
-        ahead(c)
-    lines = group_lines(modes_ref, row_back_ref[0], span)
-    for c in range(block // 2):
-        cell(c, lines[c])
-    finish(jnp.maximum(step - 1, 0))
-    for c in range(block // 2, block):
-        cell(c, lines[c])
+        if c % 2 == 0:
+            ahead(c)
+        cell(c, held_ref[c])
+        if c == 0:
+            finish(made_ref, jnp.maximum(step - 2, 0))
+        if c == 1:
+            prepare(jnp.minimum(step + 1, pl.num_programs(0) - 1))
 
     @pl.when(step == pl.num_programs(0) - 1)
     def _():
-        for c in range(block):
+        finish(lines_ref, step - 1)
+        for c in range(0, block, 2):
             ahead(c)
-        finish(step)
+        finish(lines_ref, step)
 
 
 def last_packed(
@@ -590,13 +612,14 @@
 ):
     block = out_ref.shape[0]
     step = pl.program_id(0)
-    lines = group_lines(modes_ref, row_back_ref[0], span)
+    lines = group_lines(modes_ref, step, kx, row_back_ref[0], span)
     count, freqs, outs = wgrad_ref.shape[0], wgrad_ref.shape[1], wgrad_ref.shape[4]
     wide = freqs * kx
     first = lax.axis_index("chan") * (count * pl.num_programs(0)) + step * count
     g_real, g_imag = both_parts(grads_ref, slice(None))
+    limit = column_of(limit_ref[...], outs, 0)
     for i in range(count):
-        keep = jnp.broadcast_to(limit_ref[:, :1], (outs, wide)) > first + i
+        keep = jnp.broadcast_to(limit, (outs, wide)) > (first + i).astype(jnp.float32)
         s_real, s_imag = both_parts(spec_ref, pl.ds(step * count + i, 1))
         real = jnp.where(keep, s_real * g_real + s_imag * g_imag, 0.0)
         imag = jnp.where(keep, s_real * g_imag - s_imag * g_real, 0.0)
@@ -661,6 +684,29 @@
     )
     copy.start()
     return copy
+
+
+def column_of(row, count, first):
+    shape = (count, row.shape[1])
+    hit = lanes_of(shape) == first + lax.broadcasted_iota(jnp.int32, shape, 0)
+    return jnp.sum(jnp.where(hit, row.astype(jnp.float32), 0.0), axis=1, keepdims=True)
+
+
+def mode_scales(limit_ref, shape, kx, cells_total):
+    wide, count, _ = shape
+    first = lax.axis_index("chan") * count
+    cols = jnp.broadcast_to(column_of(limit_ref[0:1], count, first), (count, LANES))
+    rows = jnp.broadcast_to(column_of(limit_ref[1:2], count, first), (count, LANES))
+    all_kx = (kx * lax.axis_size("slab"))
+    tiles = []
+    for j in range(wide):
+        cell = lanes_of((count, LANES)) + j * LANES
+        col = (lax.axis_index("mode") * (wide * LANES // kx) + cell // kx).astype(jnp.float32)
+        row = (lax.axis_index("slab") * kx + cell % kx).astype(jnp.float32)
+        kept = (col < cols) & ((row < rows) | (all_kx - row < rows))
+        scale = jnp.where(col < 0.5, 1.0, 2.0) / cells_total
+        tiles.append(jnp.where(kept, scale, 0.0)[None])
+    return jnp.concatenate(tiles, axis=0)
 
 
 def greet(slabs):
@@ -736,7 +782,7 @@
 
 
 def forward_kernel(
-    span, slabs, kx, x_ref, ahead_ref, row_ref, w_ref, limit_ref, weight_ref, out_ref, turned_ref, spec_ref, x_buf,
+    span, slabs, kx, x_ref, ahead_ref, row_ref, w_ref, limit_ref, mode_limit_ref, out_ref, turned_ref, spec_ref, x_buf, kept_ref,
     part_ref, half_ref, give_ref, take_ref, w_buf, t_buf, sum_ref, peer_ref, own_ref, lines_ref, ahead_buf, row_buf,
     mode_a, slab_a, mode_b, slab_b, chan_sems, x_sems, w_sems, table_sems, t_sems,
 ):
@@ -768,9 +814,8 @@
         x_copy(2 * g + 1).start()
         if g == 0:
             tables[1].start()
-        if g > 0:
-            w_copy(g - 1).start()
-    w_copy(groups - 1).start()
+    for g in range(groups):
+        w_copy(g).start()
     greet(slabs)
 
     def t_copy(g):
@@ -805,10 +850,12 @@
             part_ref[owner, place(g)] = values
         mix_rows(lines_ref, row_buf[...], rows, span, kx, store)
 
+    limit = column_of(limit_ref[...], outs, 0)
+
     def flip(g):
         for k in range(block):
             i = g * block + k
-            keep = jnp.broadcast_to(limit_ref[:, :1], (outs, wide)) > first + i
+            keep = jnp.broadcast_to(limit, (outs, wide)) > (first + i).astype(jnp.float32)
             for p in range(2):
                 turned = w_buf[i, :, p].reshape(wide, outs).T
                 t_buf[i, :, p * wide : (p + 1) * wide] = jnp.where(keep, turned, 0.0)
@@ -825,11 +872,8 @@
     ahead(0)
 
     def body(g, carry):
-        w_copy(g - 1).wait()
         finish(g - 1)
-        flip(g - 1)
         ahead(g)
-        t_copy(g - 1).start()
         mode_copy(g - 1).start()
 
         @pl.when(g > 1)
@@ -838,13 +882,18 @@
         return carry
 
     lax.fori_loop(1, groups, body, 0)
-    w_copy(groups - 1).wait()
     finish(groups - 1)
     mode_copy(groups - 1).start()
     pass_on(groups - 2)
-    flip(groups - 1)
-    t_copy(groups - 1).start()
     pass_on(groups - 1)
+    kept_ref[...] = mode_scales(mode_limit_ref, kept_ref.shape, kx, slabs * rows * 2 * cols)
+
+    def turn_over(g, carry):
+        w_copy(g).wait()
+        flip(g)
+        t_copy(g).start()
+        return carry
+    lax.fori_loop(0, groups, turn_over, 0)
     mine = part_ref[me_mode * slabs + me_slab] + half_ref[me_slab]
 
     def landed(g, carry):
@@ -872,7 +921,7 @@
     )
     swap.wait_recv()
     for j in range(peer_ref.shape[0]):
-        peer_ref[j] = (sum_ref[j, pl.ds(first, mine_outs)] + peer_ref[j]) * weight_ref[j % weight_ref.shape[0]]
+        peer_ref[j] = (sum_ref[j, pl.ds(first, mine_outs)] + peer_ref[j]) * kept_ref[j % kept_ref.shape[0]]
     own_ref[...] = to_rows(peer_ref, mine_outs // 8, kx)
     state = gather_start(own_ref, out_ref, mode_b, slab_b, slabs)
     gather_finish(state, out_ref, mode_b, slabs, lambda k: None)
@@ -969,30 +1018,18 @@
     ahead, row_ahead, row_behind, behind = (
         jnp.asarray(t) for t in packed_tables(all_rows, all_cols, slabs, modes, freqs, all_kx)
     )
-    slab_index, mode_index, chan_index = (lax.axis_index(axis) for axis in ("slab", "mode", "chan"))
 
     def pick(table, axis):
         return pl.BlockSpec((1,) + table.shape[1:], lambda g: (lax.axis_index(axis), 0, 0))
 
     cells = pl.BlockSpec((block, rows, cols), lambda g: (g, 0, 0))
-    freq_cells = pl.BlockSpec((owners, 1, kx, LANES), lambda g: (0, g, 0, 0))
     scalars = pl.BlockSpec(memory_space=pltpu.SMEM)
     field = jax.ShapeDtypeStruct(source_field.shape, jnp.float32)
-    freq_field = jax.ShapeDtypeStruct((owners, groups, kx, LANES), jnp.float32)
     room = lambda size: pltpu.CompilerParams(dimension_semantics=("arbitrary",), vmem_limit_bytes=size * MIB)
     f32 = jnp.float32
 
     weight = spectral_weight.transpose(0, 2, 3, 4, 1)
-    col_freq = mode_index * freqs + jnp.arange(freqs, dtype=jnp.int32)
-    row_freq = slab_index * kx + jnp.arange(kx, dtype=jnp.int32)
-    limit_rows = lax.dynamic_slice_in_dim(mode_limit, chan_index * channels, channels, 0)
-    flat_cols, flat_rows = jnp.repeat(col_freq, kx)[None, :], jnp.tile(row_freq, freqs)[None, :]
-    kept = (flat_cols < limit_rows[:, 0:1]) & (
-        (flat_rows < limit_rows[:, 1:2]) | (all_kx - flat_rows < limit_rows[:, 1:2])
-    )
-    scales = jnp.where(flat_cols == 0, 1.0, 2.0).astype(jnp.float32) / (all_rows * all_cols)
-    weights = jnp.where(kept, scales, 0.0).reshape(channels, -1, LANES).transpose(1, 0, 2)
-    limit = jnp.broadcast_to(width_limit[:, None], (outs, LANES))
+    limit = width_limit.reshape(1, outs)
 
     dma, vmem = pltpu.SemaphoreType.DMA, pltpu.VMEM
     in_vmem, anywhere = pl.BlockSpec(memory_space=pltpu.VMEM), pl.BlockSpec(memory_space=pl.ANY)
@@ -1007,13 +1044,14 @@
     in_hbm = lambda array: pltpu.with_memory_space_constraint(array, pltpu.HBM)
     held = lambda array: pltpu.with_memory_space_constraint(array, pltpu.VMEM)
     modes_shape = (owners,) + piece
-    out_modes, turned, spec, source_held = pl.pallas_call(
+    out_modes, turned, spec, source_held, weights = pl.pallas_call(
         functools.partial(forward_kernel, span, slabs, kx),
         in_specs=[anywhere, anywhere, anywhere, anywhere, in_vmem, in_vmem],
-        out_specs=[in_vmem, anywhere, in_vmem, in_vmem],
+        out_specs=[in_vmem, anywhere, in_vmem, in_vmem, in_vmem],
         out_shape=[
             jax.ShapeDtypeStruct(modes_shape, f32), pltpu.HBM((channels, outs, 2 * wide), f32),
             jax.ShapeDtypeStruct(flat(channels), f32), pltpu.VMEM(field.shape, f32),
+            jax.ShapeDtypeStruct((wide // LANES, channels, LANES), f32),
         ],
         scratch_shapes=[vmem(modes_shape, f32)] + common + [
             vmem(weight.shape, f32), vmem((channels, outs, 2 * wide), f32), vmem(flat(outs), f32), vmem(flat(outs // 2), f32), vmem(piece, f32),
@@ -1023,23 +1061,26 @@
         ],
         compiler_params=comm(20, FORWARD),
         name="forward_modes",
-    )(in_hbm(source_field), in_hbm(ahead), in_hbm(row_ahead), in_hbm(weight), limit, weights)
+    )(in_hbm(source_field), in_hbm(ahead), in_hbm(row_ahead), in_hbm(weight), limit, mode_limit.T)
 
     output, grad_sum, grad_partial, sums = pl.pallas_call(
-        functools.partial(middle_packed, span),
+        functools.partial(middle_packed, span, kx),
         grid=(groups,),
         in_specs=[
-            in_vmem, cells, freq_cells, scalars, scalars, pick(ahead, "mode"), pick(row_ahead, "slab"),
+            in_vmem, cells, in_vmem, scalars, scalars, pick(ahead, "mode"), pick(row_ahead, "slab"),
             pick(row_behind, "slab"), pick(behind, "mode"),
         ],
         out_specs=[cells, in_vmem, in_vmem, in_vmem],
         out_shape=[field, pltpu.VMEM(field.shape, f32), jax.ShapeDtypeStruct(modes_shape, f32), jax.ShapeDtypeStruct((8, LANES), f32)],
-        scratch_shapes=[vmem((block * rows, 2 * cols), jnp.bfloat16), vmem((block * rows, LANES), f32)],
+        scratch_shapes=[
+            vmem((block * rows, 2 * cols), jnp.bfloat16), vmem((block * rows, LANES), f32), vmem((block, rows, cols), f32),
+            vmem((block, rows, LANES), f32), vmem((block, rows, LANES), f32), vmem((block * rows, LANES), f32),
+        ],
         input_output_aliases={0: 1},
         compiler_params=room(MIDDLE),
         name="middle",
     )(
-        held(source_held), cotangent, out_modes.reshape(freq_field.shape), skip_gain, channel_bias,
+        held(source_held), cotangent, out_modes, skip_gain, channel_bias,
         ahead, row_ahead, row_behind, behind,
     )
 
@@ -1052,7 +1093,7 @@
             vmem((channels, outs, 2 * wide), f32), vmem(flat(channels), f32), vmem(piece, f32), vmem((8, LANES), f32),
             vmem((slabs, 8, LANES), f32), vmem((8, LANES), f32),
         ] + pair + [dma((2,)), dma((2,)), dma((2, slabs)), dma],
-        compiler_params=comm(21, 20),
+        compiler_params=comm(21, BACKWARD),
         name="backward_modes",
     )(grad_partial, sums, in_hbm(turned), weights)
 
@@ -1062,7 +1103,7 @@
         functools.partial(last_packed, span, kx),
         grid=(groups,),
         in_specs=[
-            in_vmem, freq_cells, scalars, pick(row_behind, "slab"), pick(behind, "mode"),
+            in_vmem, in_vmem, scalars, pick(row_behind, "slab"), pick(behind, "mode"),
             whole(all_grads), whole(spec), whole(limit),
         ],
         out_specs=[cells, pl.BlockSpec((count,) + weight.shape[1:], lambda g: (g, 0, 0, 0, 0))],
@@ -1070,7 +1111,7 @@
         compiler_params=room(LAST),
         name="last",
     )(
-        pltpu.with_memory_space_constraint(grad_sum, pltpu.VMEM), back_modes.reshape(freq_field.shape), skip_gain,
+        pltpu.with_memory_space_constraint(grad_sum, pltpu.VMEM), back_modes, skip_gain,
         row_behind, behind, all_grads, spec, limit,
     )
     spectral_grad = weight_grad.transpose(0, 4, 1, 2, 3)

time: 114 us -> 106 us (0.930)
  Pallas kernels: 107 us -> 102 us
  local copies, waits for them, and re-layouts: 6 us -> 3.68 us
    pallas_call x1, Pallas kernels: 29.1 us -> 26.6 us  [local(): pl.pallas_call(functools.partial(middle_packed, span, kx), grid=(groups,)...]
    broadcast_in_dim x3 -> x0, local copies, waits for them, and re-layouts: 1.49 us -> none  [the longest x1 1.34 us: local(): limit = jnp.broadcast_to(width_limit[:, None], (outs, LANES))]
    pallas_call x1, Pallas kernels: 23.6 us -> 22.3 us  [local(): pl.pallas_call(functools.partial(backward_kernel, slabs, kx), in_specs=[i...]
    unnamed x14 -> x10, local copies, waits for them, and re-layouts: 3.83 us -> 3.16 us
where the time goes in v4:
time: 106 us
  Pallas kernels  102 us (96%)
  local copies, waits for them, and re-layouts  3.68 us (3%)
    pallas_call x1, Pallas kernels, local(): pl.pallas_call(functools.partial(forward_kernel, span, slabs, kx), in_spe...  40.7 us
    pallas_call x1, Pallas kernels, local(): pl.pallas_call(functools.partial(middle_packed, span, kx), grid=(groups,)...  26.6 us
    pallas_call x1, Pallas kernels, local(): pl.pallas_call(functools.partial(backward_kernel, slabs, kx), in_specs=[i...  22.3 us
    pallas_call x1, Pallas kernels, local(): pl.pallas_call(functools.partial(last_packed, span, kx), grid=(groups,),...  12.2 us
    unnamed x10, local copies, waits for them, and re-layouts  3.16 us

profile of v4, /device:TPU:0, one launch (start us, length us, event | category | flops | bytes accessed | tf_op | source)
XLA Modules:
  0.0 106.1 jit_solution(13252503758353011648)
XLA Ops:
  0.6 40.7 %forward_modes.1 = (f32[8,128,128]{2,1,0:T(8,128)}, f32[32,64,512]{2,1,0:T(8,128)}, f32[4,32,128]{2,1,0:T(8,128)}, f32[32,256,512]{2,1,0:T(8,128)S(1)}, f32[2,32,128]{2,1,0:T(8,128)}) custom-call(f32[32,256,512]{2,1,0:T(8,128)} %x_ref.1, bf16[2,512,128]{2,1,0:T(8,128)(2,1)} %constant.8.clone.ahead_ref, bf16[4,128,512]{2,1,0:T(8,128)(2,1)} %constant.9.clone.row_ref, ...), custom_call_target="tpu_custom_call" | custom-call | tf_op jit(solution)/shard_map/forward_modes/pallas_call | solution.py:1047
  41.3 0.0 copy-start.3
  41.3 26.6 %middle.1 = (f32[32,256,512]{2,1,0:T(8,128)}, f32[32,256,512]{2,1,0:T(8,128)S(1)}, f32[8,128,128]{2,1,0:T(8,128)}, f32[8,128]{1,0:T(8,128)}) custom-call(f32[32,256,512]{2,1,0:T(8,128)S(1)} %get-tuple-element.19.x_ref, f32[32,256,512]{2,1,0:T(8,128)} %cot_ref.1, f32[8,128,128]{2,1,0:T(8,128)} %get-tuple-element.20.modes_ref, ...), custom_call_target="tpu_custom_call", output_to_operand_aliasing={{1}: (0, {})} | custom-call | tf_op jit(solution)/shard_map/middle/pallas_call | solution.py:1066
  67.9 0.0 copy-done.3
  67.9 0.0 copy-start.1
  67.9 1.0 copy-done.1
  69.0 0.0 copy-start.4
  69.0 0.7 copy-done.4
  69.6 22.3 %backward_modes.1 = (f32[8,128,128]{2,1,0:T(8,128)S(1)}, f32[4,64,128]{2,1,0:T(8,128)S(1)}, f32[8,128]{1,0:T(8,128)S(1)}) custom-call(f32[8,128,128]{2,1,0:T(8,128)S(1)} %copy-done.1, f32[8,128]{1,0:T(8,128)S(1)} %copy-done.4, f32[32,64,512]{2,1,0:T(8,128)} %get-tuple-element.25.turned_ref, f32[2,32,128]{2,1,0:T(8,128)S(1)} %copy-done.3), custom_call_target="tpu_custom_call" | custom-call | tf_op jit(solution)/shard_map/backward_modes/pallas_call | solution.py:1087
  91.9 0.0 copy-start
  91.9 0.8 copy-done
  92.7 0.0 copy-start.2
  92.7 0.6 copy-done.2
  93.4 0.5 slice_bitcast_fusion
  93.9 12.2 %last.1 = (f32[32,256,512]{2,1,0:T(8,128)}, f32[32,16,2,16,64]{4,3,2,1,0:T(8,128)}) custom-call(f32[32,256,512]{2,1,0:T(8,128)S(1)} %get-tuple-element.22.grad_ref, f32[8,128,128]{2,1,0:T(8,128)} %copy-done, f32[32]{0:T(128)} %gain_ref.3, bf16[4,256,256]{2,1,0:T(8,128)(2,1)} %constant.10.clone.row_back_ref, bf16[2,128,512]{2,1,0:T(8,128)(2,1)} %constant.11.clone.behind_ref, ...), custom_call_target="tpu_custom_call" | custom-call | tf_op jit(solution)/shard_map/last/pallas_call | solution.py:1102
Async XLA Ops:
  41.3 26.6 %copy-start.3 = (f32[2,32,128]{2,1,0:T(8,128)S(1)}, f32[2,32,128]{2,1,0:T(8,128)}, u32[]{:S(2)}) copy-start(f32[2,32,128]{2,1,0:T(8,128)} %get-tuple-element.26.weight_ref) | copy-start | bytes 98308
  67.9 1.0 copy-start.1
  69.0 0.7 copy-start.4
  91.9 0.8 copy-start
  92.7 0.6 copy-start.2

commit v5 on v4

--- a/solution.py
+++ b/solution.py
@@ -809,13 +809,11 @@
         here = pl.ds(g * block, block)
         return pltpu.make_async_copy(w_ref.at[here], w_buf.at[here], w_sems.at[g])
 
-    for g in range(groups):
+    for g in range(2):
         x_copy(2 * g).start()
         x_copy(2 * g + 1).start()
         if g == 0:
             tables[1].start()
-    for g in range(groups):
-        w_copy(g).start()
     greet(slabs)
 
     def t_copy(g):
@@ -842,6 +840,16 @@
     def ahead(g):
         x_copy(2 * g).wait()
         x_copy(2 * g + 1).wait()
+
+        @pl.when(g + 2 < groups)
+        def _():
+            x_copy(2 * g + 4).start()
+            x_copy(2 * g + 5).start()
+
+        @pl.when(g + 2 >= groups)
+        def _():
+            for k in range(groups // 2):
+                w_copy((g + 2 - groups) * (groups // 2) + k).start()
         values = x_buf[pl.ds(g * block, block)].reshape(block * rows, cols)
         lines_ref[...] = two_way(values, ahead_buf[...])
 
@@ -1088,14 +1096,14 @@
         functools.partial(backward_kernel, slabs, kx),
         in_specs=[in_vmem, in_vmem, anywhere, in_vmem],
         out_specs=[in_vmem] * 3,
-        out_shape=[jax.ShapeDtypeStruct(modes_shape, f32), jax.ShapeDtypeStruct(flat(outs), f32), jax.ShapeDtypeStruct((8, LANES), f32)],
+        out_shape=[pltpu.HBM(modes_shape, f32), pltpu.HBM(flat(outs), f32), jax.ShapeDtypeStruct((8, LANES), f32)],
         scratch_shapes=common + [
             vmem((channels, outs, 2 * wide), f32), vmem(flat(channels), f32), vmem(piece, f32), vmem((8, LANES), f32),
             vmem((slabs, 8, LANES), f32), vmem((8, LANES), f32),
         ] + pair + [dma((2,)), dma((2,)), dma((2, slabs)), dma],
         compiler_params=comm(21, BACKWARD),
         name="backward_modes",
-    )(grad_partial, sums, in_hbm(turned), weights)
+    )(in_hbm(grad_partial), in_hbm(sums), in_hbm(turned), in_hbm(weights))
 
     count = channels // groups
     whole = lambda array: pl.BlockSpec(array.shape, lambda g: (0,) * array.ndim)

time: 106 us -> 99.1 us (0.935)
  Pallas kernels: 102 us -> 97.7 us
  local copies, waits for them, and re-layouts: 3.68 us -> 0.52 us
    pallas_call x1, Pallas kernels: 40.7 us -> 34.5 us  [local(): pl.pallas_call(functools.partial(forward_kernel, span, slabs, kx), in_spe...]
    unnamed x10 -> x0, local copies, waits for them, and re-layouts: 3.16 us -> none
    pallas_call x1, Pallas kernels: 22.3 us -> 24.4 us  [local(): pl.pallas_call(functools.partial(backward_kernel, slabs, kx), in_specs=[i...]
where the time goes in v5:
time: 99.1 us; the launch traced here: 98.9 us
  Pallas kernels  97.7 us (99%)
    pallas_call x1, Pallas kernels, local(): pl.pallas_call(functools.partial(forward_kernel, span, slabs, kx), in_spe...  34.5 us
    pallas_call x1, Pallas kernels, local(): pl.pallas_call(functools.partial(middle_packed, span, kx), grid=(groups,)...  26.6 us
    pallas_call x1, Pallas kernels, local(): pl.pallas_call(functools.partial(backward_kernel, slabs, kx), in_specs=[i...  24.4 us
    pallas_call x1, Pallas kernels, local(): pl.pallas_call(functools.partial(last_packed, span, kx), grid=(groups,),...  12.2 us

profile of v5, /device:TPU:0, one launch (start us, length us, event | category | flops | bytes accessed | tf_op | source)
XLA Modules:
  0.0 98.9 jit_solution(11231965375683350337)
XLA Ops:
  0.6 34.5 %forward_modes.1 = (f32[8,128,128]{2,1,0:T(8,128)}, f32[32,64,512]{2,1,0:T(8,128)}, f32[4,32,128]{2,1,0:T(8,128)}, f32[32,256,512]{2,1,0:T(8,128)S(1)}, f32[2,32,128]{2,1,0:T(8,128)}) custom-call(f32[32,256,512]{2,1,0:T(8,128)} %x_ref.1, bf16[2,512,128]{2,1,0:T(8,128)(2,1)} %constant.8.clone.ahead_ref, bf16[4,128,512]{2,1,0:T(8,128)(2,1)} %constant.9.clone.row_ref, ...), custom_call_target="tpu_custom_call" | custom-call | tf_op jit(solution)/shard_map/forward_modes/pallas_call | solution.py:1055
  35.2 26.6 %middle.1 = (f32[32,256,512]{2,1,0:T(8,128)}, f32[32,256,512]{2,1,0:T(8,128)S(1)}, f32[8,128,128]{2,1,0:T(8,128)}, f32[8,128]{1,0:T(8,128)}) custom-call(f32[32,256,512]{2,1,0:T(8,128)S(1)} %get-tuple-element.19.x_ref, f32[32,256,512]{2,1,0:T(8,128)} %cot_ref.1, f32[8,128,128]{2,1,0:T(8,128)} %get-tuple-element.20.modes_ref, ...), custom_call_target="tpu_custom_call", output_to_operand_aliasing={{1}: (0, {})} | custom-call | tf_op jit(solution)/shard_map/middle/pallas_call | solution.py:1074
  61.7 24.4 %backward_modes.1 = (f32[8,128,128]{2,1,0:T(8,128)}, f32[4,64,128]{2,1,0:T(8,128)}, f32[8,128]{1,0:T(8,128)S(1)}) custom-call(f32[8,128,128]{2,1,0:T(8,128)} %get-tuple-element.23.part_ref, f32[8,128]{1,0:T(8,128)} %get-tuple-element.24.sums_ref, f32[32,64,512]{2,1,0:T(8,128)} %get-tuple-element.25.turned_ref, f32[2,32,128]{2,1,0:T(8,128)} %get-tuple-element.26.weight_ref), custom_call_target="tpu_custom_call" | custom-call | tf_op jit(solution)/shard_map/backward_modes/pallas_call | solution.py:1095
  86.2 0.5 slice_bitcast_fusion
  86.7 12.2 %last.1 = (f32[32,256,512]{2,1,0:T(8,128)}, f32[32,16,2,16,64]{4,3,2,1,0:T(8,128)}) custom-call(f32[32,256,512]{2,1,0:T(8,128)S(1)} %get-tuple-element.22.grad_ref, f32[8,128,128]{2,1,0:T(8,128)} %get-tuple-element.27.modes_ref, f32[32]{0:T(128)} %gain_ref.3, bf16[4,256,256]{2,1,0:T(8,128)(2,1)} %constant.10.clone.row_back_ref, ...), custom_call_target="tpu_custom_call" | custom-call | tf_op jit(solution)/shard_map/last/pallas_call | solution.py:1110

commit v6 on v5

--- a/solution.py
+++ b/solution.py
@@ -13,6 +13,7 @@
 LANES = 128
 BIG = 60 * 1024 * 1024
 MIB = 1024 * 1024
+CHUNKS = 4
 FORWARD, MIDDLE, LAST, BACKWARD = 40, 40, 40, 20
 
 
@@ -608,7 +609,8 @@
 
 
 def last_packed(
-    span, kx, grad_ref, modes_ref, gain_ref, row_back_ref, behind_ref, grads_ref, spec_ref, limit_ref, out_ref, wgrad_ref
+    span, kx, grad_ref, modes_ref, gain_ref, row_back_ref, behind_ref, grads_ref, spec_ref, limit_ref, total_ref,
+    out_ref, wgrad_ref, gate_ref, bias_ref,
 ):
     block = out_ref.shape[0]
     step = pl.program_id(0)
@@ -616,6 +618,8 @@
     count, freqs, outs = wgrad_ref.shape[0], wgrad_ref.shape[1], wgrad_ref.shape[4]
     wide = freqs * kx
     first = lax.axis_index("chan") * (count * pl.num_programs(0)) + step * count
+    gate_ref[...] = total_ref[0:1, : gate_ref.shape[1]]
+    bias_ref[...] = total_ref[1:2, : bias_ref.shape[1]]
     g_real, g_imag = both_parts(grads_ref, slice(None))
     limit = column_of(limit_ref[...], outs, 0)
     for i in range(count):
@@ -719,30 +723,39 @@
     pl.semaphore_wait(barrier, len(targets))
 
 
+def far_first(slabs):
+    return [slabs // 2] + [step for step in range(1, slabs) if step != slabs // 2]
+
+
+def chunk(rows, k):
+    size = rows // CHUNKS
+    return pl.ds(k * size, size)
+
+
 def scatter_sum(part_ref, half_ref, give_ref, take_ref, mode_sems, slab_sems, slabs, between):
     me_mode, me_slab = lax.axis_index("mode"), lax.axis_index("slab")
     peer = other("mode", 1, 2)
-    order = [slabs // 2] + [step for step in range(1, slabs) if step != slabs // 2] + [0]
+    rows = part_ref.shape[1]
     copies = []
-    for step in order:
-        slab = other("slab", step, slabs)
+    for k in range(CHUNKS):
+        here = chunk(rows, k)
         copies.append(send(
-            part_ref.at[peer * slabs + slab], half_ref.at[step], mode_sems.at[0, step], mode_sems.at[1, step], "mode", peer
+            part_ref.at[pl.ds(peer * slabs, slabs), here], half_ref.at[:, here],
+            mode_sems.at[0, 0, k], mode_sems.at[1, 0, k], "mode", peer,
         ))
-    waits = list(copies)
     out = []
-    for step, copy in zip(order, copies):
-        copy.wait_recv()
-        slab = other("slab", step, slabs)
-        total = part_ref[me_mode * slabs + slab] + half_ref[step]
-        if step == 0:
-            mine = total
-        else:
-            give_ref[step] = total
+    for k in range(CHUNKS):
+        here = chunk(rows, k)
+        copies[k].wait_recv()
+        for step in far_first(slabs):
+            slab = other("slab", step, slabs)
+            give_ref[step, here] = part_ref[me_mode * slabs + slab, here] + half_ref[slab, here]
             out.append(send(
-                give_ref.at[step], take_ref.at[step], slab_sems.at[0, step], slab_sems.at[1, step], "slab", slab
+                give_ref.at[step, here], take_ref.at[step, here],
+                slab_sems.at[0, step, k], slab_sems.at[1, step, k], "slab", slab,
             ))
     between()
+    mine = part_ref[me_mode * slabs + me_slab] + half_ref[me_slab]
     for copy in out:
         copy.wait_recv()
     for step in range(1, slabs):
@@ -750,35 +763,36 @@
     return mine, [copy.wait_send for copy in copies + out]
 
 
-def gather_start(own_ref, out_ref, mode_sems, slab_sems, slabs):
+def gather(own_ref, out_ref, mode_sems, slab_sems, slabs):
     me = lax.axis_index("mode") * slabs + lax.axis_index("slab")
-    copies = []
-    for step in [slabs // 2] + [step for step in range(1, slabs) if step != slabs // 2]:
-        copies.append(send(
-            own_ref, out_ref.at[me], slab_sems.at[0, step], slab_sems.at[1, step], "slab", other("slab", step, slabs)
-        ))
-    near = send(own_ref, out_ref.at[me], mode_sems.at[0, 0], mode_sems.at[1, 0], "mode", other("mode", 1, 2))
+    rows = own_ref.shape[0]
+    copies, relays = [], []
+    for k in range(CHUNKS):
+        here = chunk(rows, k)
+        for step in far_first(slabs):
+            copies.append((step, here, k, send(
+                own_ref.at[here], out_ref.at[me, here], slab_sems.at[0, step, k], slab_sems.at[1, step, k],
+                "slab", other("slab", step, slabs),
+            )))
+    near = send(
+        own_ref, out_ref.at[me], mode_sems.at[0, 0, 0], mode_sems.at[1, 0, 0], "mode", other("mode", 1, 2)
+    )
     out_ref[me] = own_ref[...]
-    return copies, near
-
-
-def gather_finish(state, out_ref, mode_sems, slabs, between):
-    copies, near = state
-    relays = []
-    order = [slabs // 2] + [step for step in range(1, slabs) if step != slabs // 2]
-    for k in list(range(1, slabs - 1)) + [0]:
-        between(k)
-        copies[k].wait_recv()
-        step = order[k]
-        source = lax.axis_index("mode") * slabs + other("slab", slabs - step, slabs)
-        relays.append(send(
-            out_ref.at[source], out_ref.at[source], mode_sems.at[0, step], mode_sems.at[1, step], "mode", other("mode", 1, 2)
-        ))
+    for k in range(CHUNKS):
+        for step in list(range(1, slabs, 2)) + list(range(2, slabs, 2)):
+            for other_step, here, other_k, copy in copies:
+                if (other_step, other_k) == (step, k):
+                    copy.wait_recv()
+                    source = lax.axis_index("mode") * slabs + other("slab", slabs - step, slabs)
+                    relays.append(send(
+                        out_ref.at[source, here], out_ref.at[source, here],
+                        mode_sems.at[0, step, k], mode_sems.at[1, step, k], "mode", other("mode", 1, 2),
+                    ))
     near.wait()
     for copy in relays:
         copy.wait()
-    for copy in copies:
-        copy.wait_send()
+    for one in copies:
+        one[3].wait_send()
 
 
 def forward_kernel(
@@ -931,8 +945,7 @@
     for j in range(peer_ref.shape[0]):
         peer_ref[j] = (sum_ref[j, pl.ds(first, mine_outs)] + peer_ref[j]) * kept_ref[j % kept_ref.shape[0]]
     own_ref[...] = to_rows(peer_ref, mine_outs // 8, kx)
-    state = gather_start(own_ref, out_ref, mode_b, slab_b, slabs)
-    gather_finish(state, out_ref, mode_b, slabs, lambda k: None)
+    gather(own_ref, out_ref, mode_b, slab_b, slabs)
     swap.wait_send()
 
     def settle(g, carry):
@@ -985,8 +998,7 @@
         return carry
     lax.fori_loop(0, ins, pull, 0)
     own_ref[...] = to_rows(back_ref, ins // 8, kx)
-    state = gather_start(own_ref, out_ref, mode_b, slab_b, slabs)
-    gather_finish(state, out_ref, mode_b, slabs, lambda k: None)
+    gather(own_ref, out_ref, mode_b, slab_b, slabs)
     total = pass_ref[...]
     for step, copy in zip(range(1, slabs), far):
         copy.wait()
@@ -1043,7 +1055,7 @@
     in_vmem, anywhere = pl.BlockSpec(memory_space=pltpu.VMEM), pl.BlockSpec(memory_space=pl.ANY)
     piece = (groups * kx, LANES)
     common = [vmem((slabs,) + piece, f32), vmem((slabs,) + piece, f32), vmem((slabs,) + piece, f32)]
-    pair = [dma((2, slabs))] * 4
+    pair = [dma((2, slabs, CHUNKS))] * 4
     comm = lambda ident, room: pltpu.CompilerParams(
         collective_id=ident, has_side_effects=True, vmem_limit_bytes=room * MIB
     )
@@ -1064,7 +1076,7 @@
         scratch_shapes=[vmem(modes_shape, f32)] + common + [
             vmem(weight.shape, f32), vmem((channels, outs, 2 * wide), f32), vmem(flat(outs), f32), vmem(flat(outs // 2), f32), vmem(piece, f32),
             vmem((block * rows, LANES), f32), vmem(ahead.shape[1:], jnp.bfloat16), vmem(row_ahead.shape[1:], jnp.bfloat16),
-            dma((2, groups)), dma((2, slabs, groups)), dma((2, slabs)), dma((2, slabs)), dma((2,)),
+            dma((2, groups)), dma((2, slabs, groups)), dma((2, slabs, CHUNKS)), dma((2, slabs, CHUNKS)), dma((2,)),
             dma((2 * groups,)), dma((groups,)), dma((2,)), dma((groups,)),
         ],
         compiler_params=comm(20, FORWARD),
@@ -1096,7 +1108,7 @@
         functools.partial(backward_kernel, slabs, kx),
         in_specs=[in_vmem, in_vmem, anywhere, in_vmem],
         out_specs=[in_vmem] * 3,
-        out_shape=[pltpu.HBM(modes_shape, f32), pltpu.HBM(flat(outs), f32), jax.ShapeDtypeStruct((8, LANES), f32)],
+        out_shape=[pltpu.HBM(modes_shape, f32), pltpu.HBM(flat(outs), f32), pltpu.HBM((8, LANES), f32)],
         scratch_shapes=common + [
             vmem((channels, outs, 2 * wide), f32), vmem(flat(channels), f32), vmem(piece, f32), vmem((8, LANES), f32),
             vmem((slabs, 8, LANES), f32), vmem((8, LANES), f32),
@@ -1106,24 +1118,25 @@
     )(in_hbm(grad_partial), in_hbm(sums), in_hbm(turned), in_hbm(weights))
 
     count = channels // groups
-    whole = lambda array: pl.BlockSpec(array.shape, lambda g: (0,) * array.ndim)
-    field_grad, weight_grad = pl.pallas_call(
+    whole = lambda array: pl.BlockSpec(array.shape, lambda g: (0,) * len(array.shape))
+    line = jax.ShapeDtypeStruct((1, channels), f32)
+    field_grad, weight_grad, gate_grad, bias_grad = pl.pallas_call(
         functools.partial(last_packed, span, kx),
         grid=(groups,),
         in_specs=[
             in_vmem, in_vmem, scalars, pick(row_behind, "slab"), pick(behind, "mode"),
-            whole(all_grads), whole(spec), whole(limit),
+            whole(all_grads), whole(spec), whole(limit), whole(totals),
         ],
-        out_specs=[cells, pl.BlockSpec((count,) + weight.shape[1:], lambda g: (g, 0, 0, 0, 0))],
-        out_shape=[field, jax.ShapeDtypeStruct(weight.shape, f32)],
+        out_specs=[cells, pl.BlockSpec((count,) + weight.shape[1:], lambda g: (g, 0, 0, 0, 0)), whole(line), whole(line)],
+        out_shape=[field, jax.ShapeDtypeStruct(weight.shape, f32), line, line],
         compiler_params=room(LAST),
         name="last",
     )(
         pltpu.with_memory_space_constraint(grad_sum, pltpu.VMEM), back_modes, skip_gain,
-        row_behind, behind, all_grads, spec, limit,
+        row_behind, behind, all_grads, spec, limit, totals,
     )
     spectral_grad = weight_grad.transpose(0, 4, 1, 2, 3)
-    return (output, field_grad, spectral_grad, totals[0, :channels], totals[1, :channels])
+    return (output, field_grad, spectral_grad, gate_grad.reshape(-1), bias_grad.reshape(-1))
 
 
 def solution(mesh):

time: 99.1 us -> 101 us (1.019)
  Pallas kernels: 97.7 us -> 99.7 us
    pallas_call x1, Pallas kernels: 24.4 us -> 25.5 us  [local(): pl.pallas_call(functools.partial(backward_kernel, slabs, kx), in_specs=[i...]
where the time goes in v6:
time: 101 us; the launch traced here: 100 us
  Pallas kernels  99.7 us (99%)
    pallas_call x1, Pallas kernels, local(): pl.pallas_call(functools.partial(forward_kernel, span, slabs, kx), in_spe...  35.4 us
    pallas_call x1, Pallas kernels, local(): pl.pallas_call(functools.partial(middle_packed, span, kx), grid=(groups,)...  26.6 us
    pallas_call x1, Pallas kernels, local(): pl.pallas_call(functools.partial(backward_kernel, slabs, kx), in_specs=[i...  25.5 us
    pallas_call x1, Pallas kernels, local(): pl.pallas_call(functools.partial(last_packed, span, kx), grid=(groups,),...  12.3 us

profile of v6, /device:TPU:0, one launch (start us, length us, event | category | flops | bytes accessed | tf_op | source)
XLA Modules:
  0.0 100.4 jit_solution(10344171780783192775)
XLA Ops:
  0.6 35.4 %forward_modes.1 = (f32[8,128,128]{2,1,0:T(8,128)}, f32[32,64,512]{2,1,0:T(8,128)}, f32[4,32,128]{2,1,0:T(8,128)}, f32[32,256,512]{2,1,0:T(8,128)S(1)}, f32[2,32,128]{2,1,0:T(8,128)}) custom-call(f32[32,256,512]{2,1,0:T(8,128)} %x_ref.1, bf16[2,512,128]{2,1,0:T(8,128)(2,1)} %constant.8.clone.ahead_ref, bf16[4,128,512]{2,1,0:T(8,128)(2,1)} %constant.9.clone.row_ref, ...), custom_call_target="tpu_custom_call" | custom-call | tf_op jit(solution)/shard_map/forward_modes/pallas_call | solution.py:1067
  36.1 26.6 %middle.1 = (f32[32,256,512]{2,1,0:T(8,128)}, f32[32,256,512]{2,1,0:T(8,128)S(1)}, f32[8,128,128]{2,1,0:T(8,128)}, f32[8,128]{1,0:T(8,128)}) custom-call(f32[32,256,512]{2,1,0:T(8,128)S(1)} %get-tuple-element.21.x_ref, f32[32,256,512]{2,1,0:T(8,128)} %cot_ref.1, f32[8,128,128]{2,1,0:T(8,128)} %get-tuple-element.22.modes_ref, ...), custom_call_target="tpu_custom_call", output_to_operand_aliasing={{1}: (0, {})} | custom-call | tf_op jit(solution)/shard_map/middle/pallas_call | solution.py:1086
  62.6 25.5 %backward_modes.1 = (f32[8,128,128]{2,1,0:T(8,128)}, f32[4,64,128]{2,1,0:T(8,128)}, f32[8,128]{1,0:T(8,128)}) custom-call(f32[8,128,128]{2,1,0:T(8,128)} %get-tuple-element.25.part_ref, f32[8,128]{1,0:T(8,128)} %get-tuple-element.26.sums_ref, f32[32,64,512]{2,1,0:T(8,128)} %get-tuple-element.27.turned_ref, f32[2,32,128]{2,1,0:T(8,128)} %get-tuple-element.28.weight_ref), custom_call_target="tpu_custom_call" | custom-call | tf_op jit(solution)/shard_map/backward_modes/pallas_call | solution.py:1107
  88.1 12.3 %last.1 = (f32[32,256,512]{2,1,0:T(8,128)}, f32[32,16,2,16,64]{4,3,2,1,0:T(8,128)}, f32[1,32]{1,0:T(1,128)}, f32[1,32]{1,0:T(1,128)}) custom-call(f32[32,256,512]{2,1,0:T(8,128)S(1)} %get-tuple-element.24.grad_ref, f32[8,128,128]{2,1,0:T(8,128)} %get-tuple-element.29.modes_ref, f32[32]{0:T(128)} %gain_ref.3, ...), custom_call_target="tpu_custom_call" | custom-call | tf_op jit(solution)/shard_map/last/pallas_call | solution.py:1123

commit v7 on v5

--- a/solution.py
+++ b/solution.py
@@ -540,8 +540,8 @@
     def ahead(c):
         here = slice(c * rows, (c + 2) * rows)
         table = ahead_ref[0]
-        high = jnp.dot(split_ref[here, :cols], table, preferred_element_type=jnp.float32)
-        lines_ref[here] = high + jnp.dot(split_ref[here, cols:], table, preferred_element_type=jnp.float32)
+        high = jnp.dot(split_ref[0, c // 2], table, preferred_element_type=jnp.float32)
+        lines_ref[here] = high + jnp.dot(split_ref[1, c // 2], table, preferred_element_type=jnp.float32)
 
     def finish(from_ref, group):
         def store(owner, values):
@@ -569,9 +569,9 @@
             grad = cot_ref[c, here] * (up + (up * (1.0 - up)) * bend)
             grad_ref[channel, here] = grad
             high, low = high_low(grad)
-            there = slice(c * rows + r, c * rows + r + 16)
-            split_ref[there, :cols] = high
-            split_ref[there, cols:] = low
+            there = slice(c % 2 * rows + r, c % 2 * rows + r + 16)
+            split_ref[0, c // 2, there] = high
+            split_ref[1, c // 2, there] = low
             both = grad * source
             gate = gate + (both[:8] + both[8:])
             bias = bias + (grad[:8] + grad[8:])
@@ -608,7 +608,8 @@
 
 
 def last_packed(
-    span, kx, grad_ref, modes_ref, gain_ref, row_back_ref, behind_ref, grads_ref, spec_ref, limit_ref, out_ref, wgrad_ref
+    span, kx, grad_ref, modes_ref, gain_ref, row_back_ref, behind_ref, grads_ref, spec_ref, limit_ref, total_ref,
+    out_ref, wgrad_ref, gate_ref, bias_ref,
 ):
     block = out_ref.shape[0]
     step = pl.program_id(0)
@@ -616,6 +617,8 @@
     count, freqs, outs = wgrad_ref.shape[0], wgrad_ref.shape[1], wgrad_ref.shape[4]
     wide = freqs * kx
     first = lax.axis_index("chan") * (count * pl.num_programs(0)) + step * count
+    gate_ref[...] = total_ref[0:1, : gate_ref.shape[1]]
+    bias_ref[...] = total_ref[1:2, : bias_ref.shape[1]]
     g_real, g_imag = both_parts(grads_ref, slice(None))
     limit = column_of(limit_ref[...], outs, 0)
     for i in range(count):
@@ -1081,7 +1084,7 @@
         out_specs=[cells, in_vmem, in_vmem, in_vmem],
         out_shape=[field, pltpu.VMEM(field.shape, f32), jax.ShapeDtypeStruct(modes_shape, f32), jax.ShapeDtypeStruct((8, LANES), f32)],
         scratch_shapes=[
-            vmem((block * rows, 2 * cols), jnp.bfloat16), vmem((block * rows, LANES), f32), vmem((block, rows, cols), f32),
+            vmem((2, block // 2, 2 * rows, cols), jnp.bfloat16), vmem((block * rows, LANES), f32), vmem((block, rows, cols), f32),
             vmem((block, rows, LANES), f32), vmem((block, rows, LANES), f32), vmem((block * rows, LANES), f32),
         ],
         input_output_aliases={0: 1},
@@ -1096,7 +1099,7 @@
         functools.partial(backward_kernel, slabs, kx),
         in_specs=[in_vmem, in_vmem, anywhere, in_vmem],
         out_specs=[in_vmem] * 3,
-        out_shape=[pltpu.HBM(modes_shape, f32), pltpu.HBM(flat(outs), f32), jax.ShapeDtypeStruct((8, LANES), f32)],
+        out_shape=[pltpu.HBM(modes_shape, f32), pltpu.HBM(flat(outs), f32), pltpu.HBM((8, LANES), f32)],
         scratch_shapes=common + [
             vmem((channels, outs, 2 * wide), f32), vmem(flat(channels), f32), vmem(piece, f32), vmem((8, LANES), f32),
             vmem((slabs, 8, LANES), f32), vmem((8, LANES), f32),
@@ -1106,24 +1109,25 @@
     )(in_hbm(grad_partial), in_hbm(sums), in_hbm(turned), in_hbm(weights))
 
     count = channels // groups
-    whole = lambda array: pl.BlockSpec(array.shape, lambda g: (0,) * array.ndim)
-    field_grad, weight_grad = pl.pallas_call(
+    whole = lambda array: pl.BlockSpec(array.shape, lambda g: (0,) * len(array.shape))
+    line = jax.ShapeDtypeStruct((1, channels), f32)
+    field_grad, weight_grad, gate_grad, bias_grad = pl.pallas_call(
         functools.partial(last_packed, span, kx),
         grid=(groups,),
         in_specs=[
             in_vmem, in_vmem, scalars, pick(row_behind, "slab"), pick(behind, "mode"),
-            whole(all_grads), whole(spec), whole(limit),
+            whole(all_grads), whole(spec), whole(limit), whole(totals),
         ],
-        out_specs=[cells, pl.BlockSpec((count,) + weight.shape[1:], lambda g: (g, 0, 0, 0, 0))],
-        out_shape=[field, jax.ShapeDtypeStruct(weight.shape, f32)],
+        out_specs=[cells, pl.BlockSpec((count,) + weight.shape[1:], lambda g: (g, 0, 0, 0, 0)), whole(line), whole(line)],
+        out_shape=[field, jax.ShapeDtypeStruct(weight.shape, f32), line, line],
         compiler_params=room(LAST),
         name="last",
     )(
         pltpu.with_memory_space_constraint(grad_sum, pltpu.VMEM), back_modes, skip_gain,
-        row_behind, behind, all_grads, spec, limit,
+        row_behind, behind, all_grads, spec, limit, totals,
     )
     spectral_grad = weight_grad.transpose(0, 4, 1, 2, 3)
-    return (output, field_grad, spectral_grad, totals[0, :channels], totals[1, :channels])
+    return (output, field_grad, spectral_grad, gate_grad.reshape(-1), bias_grad.reshape(-1))
 
 
 def solution(mesh):

time: 99.1 us -> 98.4 us (level)
  no operation moved by 1% of the time
where the time goes in v7:
time: 98.4 us; the launch traced here: 98.2 us
  Pallas kernels  97.6 us (99%)
    pallas_call x1, Pallas kernels, local(): pl.pallas_call(functools.partial(forward_kernel, span, slabs, kx), in_spe...  34.5 us
    pallas_call x1, Pallas kernels, local(): pl.pallas_call(functools.partial(middle_packed, span, kx), grid=(groups,)...  26.4 us
    pallas_call x1, Pallas kernels, local(): pl.pallas_call(functools.partial(backward_kernel, slabs, kx), in_specs=[i...  24.4 us
    pallas_call x1, Pallas kernels, local(): pl.pallas_call(functools.partial(last_packed, span, kx), grid=(groups,),...  12.3 us

profile of v7, /device:TPU:0, one launch (start us, length us, event | category | flops | bytes accessed | tf_op | source)
XLA Modules:
  0.0 98.2 jit_solution(17619517226946769550)
XLA Ops:
  0.6 34.5 %forward_modes.1 = (f32[8,128,128]{2,1,0:T(8,128)}, f32[32,64,512]{2,1,0:T(8,128)}, f32[4,32,128]{2,1,0:T(8,128)}, f32[32,256,512]{2,1,0:T(8,128)S(1)}, f32[2,32,128]{2,1,0:T(8,128)}) custom-call(f32[32,256,512]{2,1,0:T(8,128)} %x_ref.1, bf16[2,512,128]{2,1,0:T(8,128)(2,1)} %constant.8.clone.ahead_ref, bf16[4,128,512]{2,1,0:T(8,128)(2,1)} %constant.9.clone.row_ref, ...), custom_call_target="tpu_custom_call" | custom-call | tf_op jit(solution)/shard_map/forward_modes/pallas_call | solution.py:1058
  35.2 26.4 %middle.1 = (f32[32,256,512]{2,1,0:T(8,128)}, f32[32,256,512]{2,1,0:T(8,128)S(1)}, f32[8,128,128]{2,1,0:T(8,128)}, f32[8,128]{1,0:T(8,128)}) custom-call(f32[32,256,512]{2,1,0:T(8,128)S(1)} %get-tuple-element.21.x_ref, f32[32,256,512]{2,1,0:T(8,128)} %cot_ref.1, f32[8,128,128]{2,1,0:T(8,128)} %get-tuple-element.22.modes_ref, ...), custom_call_target="tpu_custom_call", output_to_operand_aliasing={{1}: (0, {})} | custom-call | tf_op jit(solution)/shard_map/middle/pallas_call | solution.py:1077
  61.5 24.4 %backward_modes.1 = (f32[8,128,128]{2,1,0:T(8,128)}, f32[4,64,128]{2,1,0:T(8,128)}, f32[8,128]{1,0:T(8,128)}) custom-call(f32[8,128,128]{2,1,0:T(8,128)} %get-tuple-element.25.part_ref, f32[8,128]{1,0:T(8,128)} %get-tuple-element.26.sums_ref, f32[32,64,512]{2,1,0:T(8,128)} %get-tuple-element.27.turned_ref, f32[2,32,128]{2,1,0:T(8,128)} %get-tuple-element.28.weight_ref), custom_call_target="tpu_custom_call" | custom-call | tf_op jit(solution)/shard_map/backward_modes/pallas_call | solution.py:1098
  86.0 12.3 %last.1 = (f32[32,256,512]{2,1,0:T(8,128)}, f32[32,16,2,16,64]{4,3,2,1,0:T(8,128)}, f32[1,32]{1,0:T(1,128)}, f32[1,32]{1,0:T(1,128)}) custom-call(f32[32,256,512]{2,1,0:T(8,128)S(1)} %get-tuple-element.24.grad_ref, f32[8,128,128]{2,1,0:T(8,128)} %get-tuple-element.29.modes_ref, f32[32]{0:T(128)} %gain_ref.3, ...), custom_call_target="tpu_custom_call" | custom-call | tf_op jit(solution)/shard_map/last/pallas_call | solution.py:1114
